TPU v7x, 8 devices: a whole 2x2x1 slice. The times are simulated.
8 devices in a mesh: batch: 1 (over z), cols: 2 (over y), rows: 4 (over x, core).
Axes of the slice: x: 2, y: 2, z: 1, core: 2. Of those that a mesh axis runs over, the one named last changes fastest.
Arguments:
- frames: bfloat16 [12, 2, 128, 64, 64], P(None, 'batch', 'rows', 'cols')
- w_x: bfloat16 [3, 3, 64, 256], replicated
- w_h: bfloat16 [3, 3, 64, 256], replicated
- gate_bias: float32 [256], replicated
- h_init: bfloat16 [2, 128, 64, 64], P('batch', 'rows', 'cols')
- c_init: float32 [2, 128, 64, 64], P('batch', 'rows', 'cols')
Outputs:
- output 1: bfloat16 [12, 2, 128, 64, 64], P(None, 'batch', 'rows', 'cols')
- output 2: float32 [2, 128, 64, 64], P('batch', 'rows', 'cols')
All inputs are finite; a program needn't handle non-finite values.
Results may differ from a plain program's by a relative error of at most 0.00176749.
Values are sent between devices in bfloat16 or wider.
A program may use at most 1 GiB of HBM per device.

v0:
```python
import jax
import jax.numpy as jnp
from jax import lax
from jax.sharding import PartitionSpec as P, NamedSharding


def edge_swap(tile_arr, halo_width, split_dim, axis_label, axis_count):
    length = tile_arr.shape[split_dim]
    low_edge = lax.slice_in_dim(tile_arr, 0, halo_width, axis=split_dim)
    high_edge = lax.slice_in_dim(tile_arr, length - halo_width, length, axis=split_dim)
    down_pairs = [(source, source + 1) for source in range(axis_count - 1)]
    up_pairs = [(source + 1, source) for source in range(axis_count - 1)]
    from_prev = lax.ppermute(high_edge, axis_label, down_pairs)
    from_next = lax.ppermute(low_edge, axis_label, up_pairs)
    return jnp.concatenate([from_prev, tile_arr, from_next], axis=split_dim)


def with_halo(tile_arr, halo_width, row_dim, row_count, col_count):
    row_ext = edge_swap(tile_arr, halo_width, row_dim, "rows", row_count)
    return edge_swap(row_ext, halo_width, row_dim + 1, "cols", col_count)


def conv_taps(padded, weights, out_rows, out_cols):
    tap_list = [padded[:, row_off:row_off + out_rows, col_off:col_off + out_cols, :] for row_off in range(3) for col_off in range(3)]
    patches = jnp.concatenate(tap_list, axis=-1)
    flat_patches = patches.reshape(-1, patches.shape[-1])
    flat_weights = weights.reshape(-1, weights.shape[-1])
    product = jnp.dot(flat_patches, flat_weights, preferred_element_type=jnp.float32)
    return product.reshape(padded.shape[0], out_rows, out_cols, -1)


def lstm_cell(gate_sum, cell_prev):
    hidden_width = cell_prev.shape[-1]
    in_gate = jax.nn.sigmoid(gate_sum[..., :hidden_width])
    forget_gate = jax.nn.sigmoid(gate_sum[..., hidden_width:2 * hidden_width])
    out_gate = jax.nn.sigmoid(gate_sum[..., 2 * hidden_width:3 * hidden_width])
    cand_gate = jnp.tanh(gate_sum[..., 3 * hidden_width:])
    cell_next = forget_gate * cell_prev + in_gate * cand_gate
    hidden_next = (out_gate * jnp.tanh(cell_next)).astype(jnp.bfloat16)
    return hidden_next, cell_next


def solution(mesh):
    row_count = mesh.shape["rows"]
    col_count = mesh.shape["cols"]
    frame_spec = P(None, "batch", "rows", "cols", None)
    state_spec = P("batch", "rows", "cols", None)

    def local_run(frames, w_x, w_h, gate_bias, h_init, c_init):
        tile_rows = h_init.shape[1]
        tile_cols = h_init.shape[2]
        frames_ext = with_halo(frames, 1, 2, row_count, col_count)

        def step_fn(state_pair, frame_ext):
            hidden, cell_state = state_pair
            hidden_ext = with_halo(hidden, 1, 1, row_count, col_count)
            gate_sum = conv_taps(frame_ext, w_x, tile_rows, tile_cols) + conv_taps(hidden_ext, w_h, tile_rows, tile_cols) + gate_bias
            hidden_next, cell_next = lstm_cell(gate_sum, cell_state)
            return (hidden_next, cell_next), hidden_next

        final_pair, all_hidden = lax.scan(step_fn, (h_init, c_init), frames_ext)
        return all_hidden, final_pair[1]

    return jax.shard_map(local_run, mesh=mesh, in_specs=(frame_spec, P(), P(), P(), state_spec, state_spec), out_specs=(frame_spec, state_spec), check_vma=False)
```

profile of v0, /device:TPU:0, one launch (start us, length us, event | category | flops | bytes accessed | tf_op | source)
XLA Modules:
  0.0 545.5 jit_solution(7176438452667858182)
XLA Ops:
  8.1 4.8 constant_dynamic-update-slice_fusion.4
  16.4 4.3 collective-permute-start.6
  22.0 6.6 %collective-permute-done.6 = bf16[12,2,34,1,64]{4,3,2,1,0:T(2,128)(2,1)S(1)} collective-permute-done((bf16[12,2,34,1,64]{4,3,2,1,0:T(2,128)(2,1)S(1)}, bf16[12,2,34,1,64]{4,3,2,1,0:T(2,128)(2,1)S(1)}, u32[]{:S(2)}, u32[]{:S(2)}) %collective-permute-start.6) | collective-permute-done | bytes 104480 | tf_op jit(solution)/shard_map/ppermute | solution.py:13
  28.6 4.7 collective-permute-done.7
  33.3 8.7 %pad_maximum_fusion.4 = bf16[12,2,34,34,64]{4,3,2,1,0:T(8,128)(2,1)} fusion(bf16[12,2,34,1,64]{4,3,2,1,0:T(2,128)(2,1)S(1)} %collective-permute-done.7, bf16[12,2,34,32,64]{4,3,2,1,0:T(8,128)(2,1)} %copy-done.4, bf16[12,2,34,1,64]{4,3,2,1,0:T(2,128)(2,1)S(1)} %collective-permute-done.6), kind=kLoop, calls=%fused_computation.40 | loop fusion | flops 10653696 | bytes 7102464 | tf_op jit(solution)/shard_map/concatenate | solution.py:15
  42.0 503.5 %while.14 = (s32[]{:T(128)}, bf16[2,32,32,64]{3,2,1,0:T(8,128)(2,1)S(1)}, f32[2,32,32,64]{3,2,1,0:T(8,128)}, bf16[12,2,32,32,64]{4,3,2,1,0:T(8,128)(2,1)}, bf16[...) while((s32[]{:T(128)}, ...), condition=%wide.region_1.2_spmd, body=%wide.region_0.1_spmd.sunk | while | flops 1215037440 | bytes 39324000 | solution.py:61
  50.4 5.3 concatenate.36
  59.2 5.1 collective-permute-start.3
  66.8 5.2 pad_maximum_fusion.8
  71.9 5.2 concatenate.37
  92.1 5.3 concatenate.36
  100.8 5.1 collective-permute-start.3
  108.4 5.2 pad_maximum_fusion.8
  113.5 5.2 concatenate.37
  124.9 4.3 collective-permute-start.1
  134.1 5.3 concatenate.36
  142.9 5.1 collective-permute-start.3
  150.4 5.2 pad_maximum_fusion.8
  155.6 5.2 concatenate.37
  167.0 4.3 collective-permute-start.1
  176.2 5.3 concatenate.36
  185.0 5.1 collective-permute-start.3
  192.5 5.2 pad_maximum_fusion.8
  197.7 5.2 concatenate.37
  209.1 4.3 collective-permute-start.1
  218.2 5.3 concatenate.36
  227.0 5.1 collective-permute-start.3
  234.6 5.2 pad_maximum_fusion.8
  239.7 5.2 concatenate.37
  251.1 4.3 collective-permute-start.1
  260.3 5.3 concatenate.36
  269.1 5.1 collective-permute-start.3
  276.6 5.2 pad_maximum_fusion.8
  281.8 5.2 concatenate.37
  293.2 4.3 collective-permute-start.1
  302.4 5.3 concatenate.36
  311.1 5.1 collective-permute-start.3
  318.7 5.2 pad_maximum_fusion.8
  323.8 5.2 concatenate.37
  335.2 4.3 collective-permute-start.1
  344.4 5.3 concatenate.36
  353.2 5.1 collective-permute-start.3
  360.7 5.2 pad_maximum_fusion.8
  365.9 5.2 concatenate.37
  377.3 4.3 collective-permute-start.1
  386.5 5.3 concatenate.36
  395.3 5.1 collective-permute-start.3
  402.8 5.2 pad_maximum_fusion.8
  408.0 5.2 concatenate.37
  419.4 4.3 collective-permute-start.1
  428.5 5.3 concatenate.36
  437.3 5.1 collective-permute-start.3
  444.9 5.2 pad_maximum_fusion.8
  450.0 5.2 concatenate.37
  461.4 4.3 collective-permute-start.1
  470.6 5.3 concatenate.36
  479.4 5.1 collective-permute-start.3
  486.9 5.2 pad_maximum_fusion.8
  492.1 5.2 concatenate.37
  503.5 4.3 collective-permute-start.1
  512.6 5.3 concatenate.36
  521.4 5.1 collective-permute-start.3
  529.0 5.2 pad_maximum_fusion.8
  534.1 5.2 concatenate.37
  (285 shorter events, 221.7 us)
Async XLA Ops:
  3.9 4.1 collective-permute-start.4
  6.7 6.1 %collective-permute-start.5 = (bf16[12,2,1,32,64]{4,3,2,1,0:T(8,128)(2,1)S(1)}, bf16[12,2,1,32,64]{4,3,2,1,0:T(8,128)(2,1)S(1)}, u32[]{:S(2)}, u32[]{:S(2)}) collective-permute-start(bf16[12,2,1,32,64]{4,3,2,1,0:T(8,128)(2,1)S(1)} %get-tuple-element.93), channel_id=1, source_target_pairs={{1,0},{2,1},{3,2},{5,4},{6,5},{7,6}} | collective-permute-start | bytes 294920 | tf_op jit(solution)/shard_map/ppermute | solution.py:14
  16.4 12.2 %collective-permute-start.6 = (bf16[12,2,34,1,64]{4,3,2,1,0:T(2,128)(2,1)S(1)}, bf16[12,2,34,1,64]{4,3,2,1,0:T(2,128)(2,1)S(1)}, u32[]{:S(2)}, u32[]{:S(2)}) collective-permute-start(bf16[12,2,34,1,64]{4,3,2,1,0:T(2,128)(2,1)S(1)} %get-tuple-element.91), channel_id=1, source_target_pairs={{0,4},{1,5},{2,6},{3,7}} | collective-permute-start | bytes 313352 | tf_op jit(solution)/shard_map/ppermute | solution.py:13
  20.7 12.6 %collective-permute-start.7 = (bf16[12,2,34,1,64]{4,3,2,1,0:T(2,128)(2,1)S(1)}, bf16[12,2,34,1,64]{4,3,2,1,0:T(2,128)(2,1)S(1)}, u32[]{:S(2)}, u32[]{:S(2)}) collective-permute-start(bf16[12,2,34,1,64]{4,3,2,1,0:T(2,128)(2,1)S(1)} %get-tuple-element.92), channel_id=1, source_target_pairs={{4,0},{5,1},{6,2},{7,3}} | collective-permute-start | bytes 313352 | tf_op jit(solution)/shard_map/ppermute | solution.py:14
  22.0 20.0 %copy-start = (bf16[2,32,32,64]{3,2,1,0:T(8,128)(2,1)S(1)}, bf16[2,32,32,64]{3,2,1,0:T(8,128)(2,1)}, u32[]{:S(2)}) copy-start(bf16[2,32,32,64]{3,2,1,0:T(8,128)(2,1)} %param.12) | copy-start | bytes 786436
  22.0 20.0 %copy-start.5 = (bf16[3,3,64,256]{3,2,1,0:T(8,128)(2,1)S(1)}, bf16[3,3,64,256]{3,2,1,0:T(8,128)(2,1)}, u32[]{:S(2)}) copy-start(bf16[3,3,64,256]{3,2,1,0:T(8,128)(2,1)} %param.9) | copy-start | bytes 884740
  22.0 20.0 %copy-start.6 = (f32[256]{0:T(256)S(1)}, f32[256]{0:T(256)}, u32[]{:S(2)}) copy-start(f32[256]{0:T(256)} %param.11) | copy-start | bytes 3076
  42.0 13.7 %collective-permute-start.1 = (bf16[2,1,32,64]{3,2,1,0:T(8,128)(2,1)S(1)}, bf16[2,1,32,64]{3,2,1,0:T(8,128)(2,1)S(1)}, u32[]{:S(2)}, u32[]{:S(2)}) collective-permute-start(bf16[2,1,32,64]{3,2,1,0:T(8,128)(2,1)S(1)} %get-tuple-element.179), channel_id=1, source_target_pairs={{0,1},{1,2},{2,3},{4,5},{5,6},{6,7}} | collective-permute-start | bytes 24584 | tf_op jit(solution)/shard_map/while/body/eval_jaxpr/ppermute | solution.py:13
  45.5 10.3 %collective-permute-start = (bf16[2,1,32,64]{3,2,1,0:T(8,128)(2,1)S(1)}, bf16[2,1,32,64]{3,2,1,0:T(8,128)(2,1)S(1)}, u32[]{:S(2)}, u32[]{:S(2)}) collective-permute-start(bf16[2,1,32,64]{3,2,1,0:T(8,128)(2,1)S(1)} %get-tuple-element.178), channel_id=1, source_target_pairs={{1,0},{2,1},{3,2},{5,4},{6,5},{7,6}} | collective-permute-start | bytes 24584 | tf_op jit(solution)/shard_map/while/body/eval_jaxpr/ppermute | solution.py:14
  57.9 8.8 %collective-permute-start.2 = (bf16[2,34,1,64]{3,2,1,0:T(2,128)(2,1)S(1)}, bf16[2,34,1,64]{3,2,1,0:T(2,128)(2,1)S(1)}, u32[]{:S(2)}, u32[]{:S(2)}) collective-permute-start(bf16[2,34,1,64]{3,2,1,0:T(2,128)(2,1)S(1)} %get-tuple-element.181), channel_id=1, source_target_pairs={{4,0},{5,1},{6,2},{7,3}} | collective-permute-start | bytes 26120 | tf_op jit(solution)/shard_map/while/body/eval_jaxpr/ppermute | solution.py:14
  59.2 7.5 %collective-permute-start.3 = (bf16[2,34,1,64]{3,2,1,0:T(2,128)(2,1)S(1)}, bf16[2,34,1,64]{3,2,1,0:T(2,128)(2,1)}, u32[]{:S(2)}, u32[]{:S(2)}) collective-permute-start(bf16[2,34,1,64]{3,2,1,0:T(2,128)(2,1)S(1)} %get-tuple-element.182), channel_id=1, source_target_pairs={{0,4},{1,5},{2,6},{3,7}} | collective-permute-start | bytes 26120 | tf_op jit(solution)/shard_map/while/body/eval_jaxpr/ppermute | solution.py:13
  77.1 2.8 copy-start.1
  83.3 14.1 %collective-permute-start.1 = (bf16[2,1,32,64]{3,2,1,0:T(8,128)(2,1)S(1)}, bf16[2,1,32,64]{3,2,1,0:T(8,128)(2,1)S(1)}, u32[]{:S(2)}, u32[]{:S(2)}) collective-permute-start(bf16[2,1,32,64]{3,2,1,0:T(8,128)(2,1)S(1)} %get-tuple-element.179), channel_id=1, source_target_pairs={{0,1},{1,2},{2,3},{4,5},{5,6},{6,7}} | collective-permute-start | bytes 24584 | tf_op jit(solution)/shard_map/while/body/eval_jaxpr/ppermute | solution.py:13
  87.2 10.3 %collective-permute-start = (bf16[2,1,32,64]{3,2,1,0:T(8,128)(2,1)S(1)}, bf16[2,1,32,64]{3,2,1,0:T(8,128)(2,1)S(1)}, u32[]{:S(2)}, u32[]{:S(2)}) collective-permute-start(bf16[2,1,32,64]{3,2,1,0:T(8,128)(2,1)S(1)} %get-tuple-element.178), channel_id=1, source_target_pairs={{1,0},{2,1},{3,2},{5,4},{6,5},{7,6}} | collective-permute-start | bytes 24584 | tf_op jit(solution)/shard_map/while/body/eval_jaxpr/ppermute | solution.py:14
  99.5 8.8 %collective-permute-start.2 = (bf16[2,34,1,64]{3,2,1,0:T(2,128)(2,1)S(1)}, bf16[2,34,1,64]{3,2,1,0:T(2,128)(2,1)S(1)}, u32[]{:S(2)}, u32[]{:S(2)}) collective-permute-start(bf16[2,34,1,64]{3,2,1,0:T(2,128)(2,1)S(1)} %get-tuple-element.181), channel_id=1, source_target_pairs={{4,0},{5,1},{6,2},{7,3}} | collective-permute-start | bytes 26120 | tf_op jit(solution)/shard_map/while/body/eval_jaxpr/ppermute | solution.py:14
  100.8 7.5 %collective-permute-start.3 = (bf16[2,34,1,64]{3,2,1,0:T(2,128)(2,1)S(1)}, bf16[2,34,1,64]{3,2,1,0:T(2,128)(2,1)}, u32[]{:S(2)}, u32[]{:S(2)}) collective-permute-start(bf16[2,34,1,64]{3,2,1,0:T(2,128)(2,1)S(1)} %get-tuple-element.182), channel_id=1, source_target_pairs={{0,4},{1,5},{2,6},{3,7}} | collective-permute-start | bytes 26120 | tf_op jit(solution)/shard_map/while/body/eval_jaxpr/ppermute | solution.py:13
  118.8 2.8 copy-start.1
  124.9 14.5 %collective-permute-start.1 = (bf16[2,1,32,64]{3,2,1,0:T(8,128)(2,1)S(1)}, bf16[2,1,32,64]{3,2,1,0:T(8,128)(2,1)S(1)}, u32[]{:S(2)}, u32[]{:S(2)}) collective-permute-start(bf16[2,1,32,64]{3,2,1,0:T(8,128)(2,1)S(1)} %get-tuple-element.179), channel_id=1, source_target_pairs={{0,1},{1,2},{2,3},{4,5},{5,6},{6,7}} | collective-permute-start | bytes 24584 | tf_op jit(solution)/shard_map/while/body/eval_jaxpr/ppermute | solution.py:13
  129.2 10.3 %collective-permute-start = (bf16[2,1,32,64]{3,2,1,0:T(8,128)(2,1)S(1)}, bf16[2,1,32,64]{3,2,1,0:T(8,128)(2,1)S(1)}, u32[]{:S(2)}, u32[]{:S(2)}) collective-permute-start(bf16[2,1,32,64]{3,2,1,0:T(8,128)(2,1)S(1)} %get-tuple-element.178), channel_id=1, source_target_pairs={{1,0},{2,1},{3,2},{5,4},{6,5},{7,6}} | collective-permute-start | bytes 24584 | tf_op jit(solution)/shard_map/while/body/eval_jaxpr/ppermute | solution.py:14
  141.6 8.8 %collective-permute-start.2 = (bf16[2,34,1,64]{3,2,1,0:T(2,128)(2,1)S(1)}, bf16[2,34,1,64]{3,2,1,0:T(2,128)(2,1)S(1)}, u32[]{:S(2)}, u32[]{:S(2)}) collective-permute-start(bf16[2,34,1,64]{3,2,1,0:T(2,128)(2,1)S(1)} %get-tuple-element.181), channel_id=1, source_target_pairs={{4,0},{5,1},{6,2},{7,3}} | collective-permute-start | bytes 26120 | tf_op jit(solution)/shard_map/while/body/eval_jaxpr/ppermute | solution.py:14
  142.9 7.5 %collective-permute-start.3 = (bf16[2,34,1,64]{3,2,1,0:T(2,128)(2,1)S(1)}, bf16[2,34,1,64]{3,2,1,0:T(2,128)(2,1)}, u32[]{:S(2)}, u32[]{:S(2)}) collective-permute-start(bf16[2,34,1,64]{3,2,1,0:T(2,128)(2,1)S(1)} %get-tuple-element.182), channel_id=1, source_target_pairs={{0,4},{1,5},{2,6},{3,7}} | collective-permute-start | bytes 26120 | tf_op jit(solution)/shard_map/while/body/eval_jaxpr/ppermute | solution.py:13
  160.8 2.8 copy-start.1
  167.0 14.5 %collective-permute-start.1 = (bf16[2,1,32,64]{3,2,1,0:T(8,128)(2,1)S(1)}, bf16[2,1,32,64]{3,2,1,0:T(8,128)(2,1)S(1)}, u32[]{:S(2)}, u32[]{:S(2)}) collective-permute-start(bf16[2,1,32,64]{3,2,1,0:T(8,128)(2,1)S(1)} %get-tuple-element.179), channel_id=1, source_target_pairs={{0,1},{1,2},{2,3},{4,5},{5,6},{6,7}} | collective-permute-start | bytes 24584 | tf_op jit(solution)/shard_map/while/body/eval_jaxpr/ppermute | solution.py:13
  171.3 10.3 %collective-permute-start = (bf16[2,1,32,64]{3,2,1,0:T(8,128)(2,1)S(1)}, bf16[2,1,32,64]{3,2,1,0:T(8,128)(2,1)S(1)}, u32[]{:S(2)}, u32[]{:S(2)}) collective-permute-start(bf16[2,1,32,64]{3,2,1,0:T(8,128)(2,1)S(1)} %get-tuple-element.178), channel_id=1, source_target_pairs={{1,0},{2,1},{3,2},{5,4},{6,5},{7,6}} | collective-permute-start | bytes 24584 | tf_op jit(solution)/shard_map/while/body/eval_jaxpr/ppermute | solution.py:14
  183.7 8.8 %collective-permute-start.2 = (bf16[2,34,1,64]{3,2,1,0:T(2,128)(2,1)S(1)}, bf16[2,34,1,64]{3,2,1,0:T(2,128)(2,1)S(1)}, u32[]{:S(2)}, u32[]{:S(2)}) collective-permute-start(bf16[2,34,1,64]{3,2,1,0:T(2,128)(2,1)S(1)} %get-tuple-element.181), channel_id=1, source_target_pairs={{4,0},{5,1},{6,2},{7,3}} | collective-permute-start | bytes 26120 | tf_op jit(solution)/shard_map/while/body/eval_jaxpr/ppermute | solution.py:14
  185.0 7.5 %collective-permute-start.3 = (bf16[2,34,1,64]{3,2,1,0:T(2,128)(2,1)S(1)}, bf16[2,34,1,64]{3,2,1,0:T(2,128)(2,1)}, u32[]{:S(2)}, u32[]{:S(2)}) collective-permute-start(bf16[2,34,1,64]{3,2,1,0:T(2,128)(2,1)S(1)} %get-tuple-element.182), channel_id=1, source_target_pairs={{0,4},{1,5},{2,6},{3,7}} | collective-permute-start | bytes 26120 | tf_op jit(solution)/shard_map/while/body/eval_jaxpr/ppermute | solution.py:13
  202.9 2.8 copy-start.1
  209.1 14.5 %collective-permute-start.1 = (bf16[2,1,32,64]{3,2,1,0:T(8,128)(2,1)S(1)}, bf16[2,1,32,64]{3,2,1,0:T(8,128)(2,1)S(1)}, u32[]{:S(2)}, u32[]{:S(2)}) collective-permute-start(bf16[2,1,32,64]{3,2,1,0:T(8,128)(2,1)S(1)} %get-tuple-element.179), channel_id=1, source_target_pairs={{0,1},{1,2},{2,3},{4,5},{5,6},{6,7}} | collective-permute-start | bytes 24584 | tf_op jit(solution)/shard_map/while/body/eval_jaxpr/ppermute | solution.py:13
  213.3 10.3 %collective-permute-start = (bf16[2,1,32,64]{3,2,1,0:T(8,128)(2,1)S(1)}, bf16[2,1,32,64]{3,2,1,0:T(8,128)(2,1)S(1)}, u32[]{:S(2)}, u32[]{:S(2)}) collective-permute-start(bf16[2,1,32,64]{3,2,1,0:T(8,128)(2,1)S(1)} %get-tuple-element.178), channel_id=1, source_target_pairs={{1,0},{2,1},{3,2},{5,4},{6,5},{7,6}} | collective-permute-start | bytes 24584 | tf_op jit(solution)/shard_map/while/body/eval_jaxpr/ppermute | solution.py:14
  225.7 8.8 %collective-permute-start.2 = (bf16[2,34,1,64]{3,2,1,0:T(2,128)(2,1)S(1)}, bf16[2,34,1,64]{3,2,1,0:T(2,128)(2,1)S(1)}, u32[]{:S(2)}, u32[]{:S(2)}) collective-permute-start(bf16[2,34,1,64]{3,2,1,0:T(2,128)(2,1)S(1)} %get-tuple-element.181), channel_id=1, source_target_pairs={{4,0},{5,1},{6,2},{7,3}} | collective-permute-start | bytes 26120 | tf_op jit(solution)/shard_map/while/body/eval_jaxpr/ppermute | solution.py:14
  227.0 7.5 %collective-permute-start.3 = (bf16[2,34,1,64]{3,2,1,0:T(2,128)(2,1)S(1)}, bf16[2,34,1,64]{3,2,1,0:T(2,128)(2,1)}, u32[]{:S(2)}, u32[]{:S(2)}) collective-permute-start(bf16[2,34,1,64]{3,2,1,0:T(2,128)(2,1)S(1)} %get-tuple-element.182), channel_id=1, source_target_pairs={{0,4},{1,5},{2,6},{3,7}} | collective-permute-start | bytes 26120 | tf_op jit(solution)/shard_map/while/body/eval_jaxpr/ppermute | solution.py:13
  244.9 2.8 copy-start.1
  251.1 14.5 %collective-permute-start.1 = (bf16[2,1,32,64]{3,2,1,0:T(8,128)(2,1)S(1)}, bf16[2,1,32,64]{3,2,1,0:T(8,128)(2,1)S(1)}, u32[]{:S(2)}, u32[]{:S(2)}) collective-permute-start(bf16[2,1,32,64]{3,2,1,0:T(8,128)(2,1)S(1)} %get-tuple-element.179), channel_id=1, source_target_pairs={{0,1},{1,2},{2,3},{4,5},{5,6},{6,7}} | collective-permute-start | bytes 24584 | tf_op jit(solution)/shard_map/while/body/eval_jaxpr/ppermute | solution.py:13
  255.4 10.3 %collective-permute-start = (bf16[2,1,32,64]{3,2,1,0:T(8,128)(2,1)S(1)}, bf16[2,1,32,64]{3,2,1,0:T(8,128)(2,1)S(1)}, u32[]{:S(2)}, u32[]{:S(2)}) collective-permute-start(bf16[2,1,32,64]{3,2,1,0:T(8,128)(2,1)S(1)} %get-tuple-element.178), channel_id=1, source_target_pairs={{1,0},{2,1},{3,2},{5,4},{6,5},{7,6}} | collective-permute-start | bytes 24584 | tf_op jit(solution)/shard_map/while/body/eval_jaxpr/ppermute | solution.py:14
  267.8 8.8 %collective-permute-start.2 = (bf16[2,34,1,64]{3,2,1,0:T(2,128)(2,1)S(1)}, bf16[2,34,1,64]{3,2,1,0:T(2,128)(2,1)S(1)}, u32[]{:S(2)}, u32[]{:S(2)}) collective-permute-start(bf16[2,34,1,64]{3,2,1,0:T(2,128)(2,1)S(1)} %get-tuple-element.181), channel_id=1, source_target_pairs={{4,0},{5,1},{6,2},{7,3}} | collective-permute-start | bytes 26120 | tf_op jit(solution)/shard_map/while/body/eval_jaxpr/ppermute | solution.py:14
  269.1 7.5 %collective-permute-start.3 = (bf16[2,34,1,64]{3,2,1,0:T(2,128)(2,1)S(1)}, bf16[2,34,1,64]{3,2,1,0:T(2,128)(2,1)}, u32[]{:S(2)}, u32[]{:S(2)}) collective-permute-start(bf16[2,34,1,64]{3,2,1,0:T(2,128)(2,1)S(1)} %get-tuple-element.182), channel_id=1, source_target_pairs={{0,4},{1,5},{2,6},{3,7}} | collective-permute-start | bytes 26120 | tf_op jit(solution)/shard_map/while/body/eval_jaxpr/ppermute | solution.py:13
  287.0 2.8 copy-start.1
  293.2 14.5 %collective-permute-start.1 = (bf16[2,1,32,64]{3,2,1,0:T(8,128)(2,1)S(1)}, bf16[2,1,32,64]{3,2,1,0:T(8,128)(2,1)S(1)}, u32[]{:S(2)}, u32[]{:S(2)}) collective-permute-start(bf16[2,1,32,64]{3,2,1,0:T(8,128)(2,1)S(1)} %get-tuple-element.179), channel_id=1, source_target_pairs={{0,1},{1,2},{2,3},{4,5},{5,6},{6,7}} | collective-permute-start | bytes 24584 | tf_op jit(solution)/shard_map/while/body/eval_jaxpr/ppermute | solution.py:13
  297.5 10.3 %collective-permute-start = (bf16[2,1,32,64]{3,2,1,0:T(8,128)(2,1)S(1)}, bf16[2,1,32,64]{3,2,1,0:T(8,128)(2,1)S(1)}, u32[]{:S(2)}, u32[]{:S(2)}) collective-permute-start(bf16[2,1,32,64]{3,2,1,0:T(8,128)(2,1)S(1)} %get-tuple-element.178), channel_id=1, source_target_pairs={{1,0},{2,1},{3,2},{5,4},{6,5},{7,6}} | collective-permute-start | bytes 24584 | tf_op jit(solution)/shard_map/while/body/eval_jaxpr/ppermute | solution.py:14
  309.8 8.8 %collective-permute-start.2 = (bf16[2,34,1,64]{3,2,1,0:T(2,128)(2,1)S(1)}, bf16[2,34,1,64]{3,2,1,0:T(2,128)(2,1)S(1)}, u32[]{:S(2)}, u32[]{:S(2)}) collective-permute-start(bf16[2,34,1,64]{3,2,1,0:T(2,128)(2,1)S(1)} %get-tuple-element.181), channel_id=1, source_target_pairs={{4,0},{5,1},{6,2},{7,3}} | collective-permute-start | bytes 26120 | tf_op jit(solution)/shard_map/while/body/eval_jaxpr/ppermute | solution.py:14
  311.1 7.5 %collective-permute-start.3 = (bf16[2,34,1,64]{3,2,1,0:T(2,128)(2,1)S(1)}, bf16[2,34,1,64]{3,2,1,0:T(2,128)(2,1)}, u32[]{:S(2)}, u32[]{:S(2)}) collective-permute-start(bf16[2,34,1,64]{3,2,1,0:T(2,128)(2,1)S(1)} %get-tuple-element.182), channel_id=1, source_target_pairs={{0,4},{1,5},{2,6},{3,7}} | collective-permute-start | bytes 26120 | tf_op jit(solution)/shard_map/while/body/eval_jaxpr/ppermute | solution.py:13
  329.1 2.8 copy-start.1
  335.2 14.5 %collective-permute-start.1 = (bf16[2,1,32,64]{3,2,1,0:T(8,128)(2,1)S(1)}, bf16[2,1,32,64]{3,2,1,0:T(8,128)(2,1)S(1)}, u32[]{:S(2)}, u32[]{:S(2)}) collective-permute-start(bf16[2,1,32,64]{3,2,1,0:T(8,128)(2,1)S(1)} %get-tuple-element.179), channel_id=1, source_target_pairs={{0,1},{1,2},{2,3},{4,5},{5,6},{6,7}} | collective-permute-start | bytes 24584 | tf_op jit(solution)/shard_map/while/body/eval_jaxpr/ppermute | solution.py:13
  339.5 10.3 %collective-permute-start = (bf16[2,1,32,64]{3,2,1,0:T(8,128)(2,1)S(1)}, bf16[2,1,32,64]{3,2,1,0:T(8,128)(2,1)S(1)}, u32[]{:S(2)}, u32[]{:S(2)}) collective-permute-start(bf16[2,1,32,64]{3,2,1,0:T(8,128)(2,1)S(1)} %get-tuple-element.178), channel_id=1, source_target_pairs={{1,0},{2,1},{3,2},{5,4},{6,5},{7,6}} | collective-permute-start | bytes 24584 | tf_op jit(solution)/shard_map/while/body/eval_jaxpr/ppermute | solution.py:14
  351.9 8.8 %collective-permute-start.2 = (bf16[2,34,1,64]{3,2,1,0:T(2,128)(2,1)S(1)}, bf16[2,34,1,64]{3,2,1,0:T(2,128)(2,1)S(1)}, u32[]{:S(2)}, u32[]{:S(2)}) collective-permute-start(bf16[2,34,1,64]{3,2,1,0:T(2,128)(2,1)S(1)} %get-tuple-element.181), channel_id=1, source_target_pairs={{4,0},{5,1},{6,2},{7,3}} | collective-permute-start | bytes 26120 | tf_op jit(solution)/shard_map/while/body/eval_jaxpr/ppermute | solution.py:14
  353.2 7.5 %collective-permute-start.3 = (bf16[2,34,1,64]{3,2,1,0:T(2,128)(2,1)S(1)}, bf16[2,34,1,64]{3,2,1,0:T(2,128)(2,1)}, u32[]{:S(2)}, u32[]{:S(2)}) collective-permute-start(bf16[2,34,1,64]{3,2,1,0:T(2,128)(2,1)S(1)} %get-tuple-element.182), channel_id=1, source_target_pairs={{0,4},{1,5},{2,6},{3,7}} | collective-permute-start | bytes 26120 | tf_op jit(solution)/shard_map/while/body/eval_jaxpr/ppermute | solution.py:13
  371.1 2.8 copy-start.1
  377.3 14.5 %collective-permute-start.1 = (bf16[2,1,32,64]{3,2,1,0:T(8,128)(2,1)S(1)}, bf16[2,1,32,64]{3,2,1,0:T(8,128)(2,1)S(1)}, u32[]{:S(2)}, u32[]{:S(2)}) collective-permute-start(bf16[2,1,32,64]{3,2,1,0:T(8,128)(2,1)S(1)} %get-tuple-element.179), channel_id=1, source_target_pairs={{0,1},{1,2},{2,3},{4,5},{5,6},{6,7}} | collective-permute-start | bytes 24584 | tf_op jit(solution)/shard_map/while/body/eval_jaxpr/ppermute | solution.py:13
  381.6 10.3 %collective-permute-start = (bf16[2,1,32,64]{3,2,1,0:T(8,128)(2,1)S(1)}, bf16[2,1,32,64]{3,2,1,0:T(8,128)(2,1)S(1)}, u32[]{:S(2)}, u32[]{:S(2)}) collective-permute-start(bf16[2,1,32,64]{3,2,1,0:T(8,128)(2,1)S(1)} %get-tuple-element.178), channel_id=1, source_target_pairs={{1,0},{2,1},{3,2},{5,4},{6,5},{7,6}} | collective-permute-start | bytes 24584 | tf_op jit(solution)/shard_map/while/body/eval_jaxpr/ppermute | solution.py:14
  394.0 8.8 %collective-permute-start.2 = (bf16[2,34,1,64]{3,2,1,0:T(2,128)(2,1)S(1)}, bf16[2,34,1,64]{3,2,1,0:T(2,128)(2,1)S(1)}, u32[]{:S(2)}, u32[]{:S(2)}) collective-permute-start(bf16[2,34,1,64]{3,2,1,0:T(2,128)(2,1)S(1)} %get-tuple-element.181), channel_id=1, source_target_pairs={{4,0},{5,1},{6,2},{7,3}} | collective-permute-start | bytes 26120 | tf_op jit(solution)/shard_map/while/body/eval_jaxpr/ppermute | solution.py:14
  395.3 7.5 %collective-permute-start.3 = (bf16[2,34,1,64]{3,2,1,0:T(2,128)(2,1)S(1)}, bf16[2,34,1,64]{3,2,1,0:T(2,128)(2,1)}, u32[]{:S(2)}, u32[]{:S(2)}) collective-permute-start(bf16[2,34,1,64]{3,2,1,0:T(2,128)(2,1)S(1)} %get-tuple-element.182), channel_id=1, source_target_pairs={{0,4},{1,5},{2,6},{3,7}} | collective-permute-start | bytes 26120 | tf_op jit(solution)/shard_map/while/body/eval_jaxpr/ppermute | solution.py:13
  419.4 14.5 %collective-permute-start.1 = (bf16[2,1,32,64]{3,2,1,0:T(8,128)(2,1)S(1)}, bf16[2,1,32,64]{3,2,1,0:T(8,128)(2,1)S(1)}, u32[]{:S(2)}, u32[]{:S(2)}) collective-permute-start(bf16[2,1,32,64]{3,2,1,0:T(8,128)(2,1)S(1)} %get-tuple-element.179), channel_id=1, source_target_pairs={{0,1},{1,2},{2,3},{4,5},{5,6},{6,7}} | collective-permute-start | bytes 24584 | tf_op jit(solution)/shard_map/while/body/eval_jaxpr/ppermute | solution.py:13
  423.6 10.3 %collective-permute-start = (bf16[2,1,32,64]{3,2,1,0:T(8,128)(2,1)S(1)}, bf16[2,1,32,64]{3,2,1,0:T(8,128)(2,1)S(1)}, u32[]{:S(2)}, u32[]{:S(2)}) collective-permute-start(bf16[2,1,32,64]{3,2,1,0:T(8,128)(2,1)S(1)} %get-tuple-element.178), channel_id=1, source_target_pairs={{1,0},{2,1},{3,2},{5,4},{6,5},{7,6}} | collective-permute-start | bytes 24584 | tf_op jit(solution)/shard_map/while/body/eval_jaxpr/ppermute | solution.py:14
  436.0 8.8 %collective-permute-start.2 = (bf16[2,34,1,64]{3,2,1,0:T(2,128)(2,1)S(1)}, bf16[2,34,1,64]{3,2,1,0:T(2,128)(2,1)S(1)}, u32[]{:S(2)}, u32[]{:S(2)}) collective-permute-start(bf16[2,34,1,64]{3,2,1,0:T(2,128)(2,1)S(1)} %get-tuple-element.181), channel_id=1, source_target_pairs={{4,0},{5,1},{6,2},{7,3}} | collective-permute-start | bytes 26120 | tf_op jit(solution)/shard_map/while/body/eval_jaxpr/ppermute | solution.py:14
  437.3 7.5 %collective-permute-start.3 = (bf16[2,34,1,64]{3,2,1,0:T(2,128)(2,1)S(1)}, bf16[2,34,1,64]{3,2,1,0:T(2,128)(2,1)}, u32[]{:S(2)}, u32[]{:S(2)}) collective-permute-start(bf16[2,34,1,64]{3,2,1,0:T(2,128)(2,1)S(1)} %get-tuple-element.182), channel_id=1, source_target_pairs={{0,4},{1,5},{2,6},{3,7}} | collective-permute-start | bytes 26120 | tf_op jit(solution)/shard_map/while/body/eval_jaxpr/ppermute | solution.py:13
  455.2 2.8 copy-start.1
  461.4 14.5 %collective-permute-start.1 = (bf16[2,1,32,64]{3,2,1,0:T(8,128)(2,1)S(1)}, bf16[2,1,32,64]{3,2,1,0:T(8,128)(2,1)S(1)}, u32[]{:S(2)}, u32[]{:S(2)}) collective-permute-start(bf16[2,1,32,64]{3,2,1,0:T(8,128)(2,1)S(1)} %get-tuple-element.179), channel_id=1, source_target_pairs={{0,1},{1,2},{2,3},{4,5},{5,6},{6,7}} | collective-permute-start | bytes 24584 | tf_op jit(solution)/shard_map/while/body/eval_jaxpr/ppermute | solution.py:13
  465.7 10.3 %collective-permute-start = (bf16[2,1,32,64]{3,2,1,0:T(8,128)(2,1)S(1)}, bf16[2,1,32,64]{3,2,1,0:T(8,128)(2,1)S(1)}, u32[]{:S(2)}, u32[]{:S(2)}) collective-permute-start(bf16[2,1,32,64]{3,2,1,0:T(8,128)(2,1)S(1)} %get-tuple-element.178), channel_id=1, source_target_pairs={{1,0},{2,1},{3,2},{5,4},{6,5},{7,6}} | collective-permute-start | bytes 24584 | tf_op jit(solution)/shard_map/while/body/eval_jaxpr/ppermute | solution.py:14
  478.1 8.8 %collective-permute-start.2 = (bf16[2,34,1,64]{3,2,1,0:T(2,128)(2,1)S(1)}, bf16[2,34,1,64]{3,2,1,0:T(2,128)(2,1)S(1)}, u32[]{:S(2)}, u32[]{:S(2)}) collective-permute-start(bf16[2,34,1,64]{3,2,1,0:T(2,128)(2,1)S(1)} %get-tuple-element.181), channel_id=1, source_target_pairs={{4,0},{5,1},{6,2},{7,3}} | collective-permute-start | bytes 26120 | tf_op jit(solution)/shard_map/while/body/eval_jaxpr/ppermute | solution.py:14
  479.4 7.5 %collective-permute-start.3 = (bf16[2,34,1,64]{3,2,1,0:T(2,128)(2,1)S(1)}, bf16[2,34,1,64]{3,2,1,0:T(2,128)(2,1)}, u32[]{:S(2)}, u32[]{:S(2)}) collective-permute-start(bf16[2,34,1,64]{3,2,1,0:T(2,128)(2,1)S(1)} %get-tuple-element.182), channel_id=1, source_target_pairs={{0,4},{1,5},{2,6},{3,7}} | collective-permute-start | bytes 26120 | tf_op jit(solution)/shard_map/while/body/eval_jaxpr/ppermute | solution.py:13
  503.5 14.5 %collective-permute-start.1 = (bf16[2,1,32,64]{3,2,1,0:T(8,128)(2,1)S(1)}, bf16[2,1,32,64]{3,2,1,0:T(8,128)(2,1)S(1)}, u32[]{:S(2)}, u32[]{:S(2)}) collective-permute-start(bf16[2,1,32,64]{3,2,1,0:T(8,128)(2,1)S(1)} %get-tuple-element.179), channel_id=1, source_target_pairs={{0,1},{1,2},{2,3},{4,5},{5,6},{6,7}} | collective-permute-start | bytes 24584 | tf_op jit(solution)/shard_map/while/body/eval_jaxpr/ppermute | solution.py:13
  507.8 10.3 %collective-permute-start = (bf16[2,1,32,64]{3,2,1,0:T(8,128)(2,1)S(1)}, bf16[2,1,32,64]{3,2,1,0:T(8,128)(2,1)S(1)}, u32[]{:S(2)}, u32[]{:S(2)}) collective-permute-start(bf16[2,1,32,64]{3,2,1,0:T(8,128)(2,1)S(1)} %get-tuple-element.178), channel_id=1, source_target_pairs={{1,0},{2,1},{3,2},{5,4},{6,5},{7,6}} | collective-permute-start | bytes 24584 | tf_op jit(solution)/shard_map/while/body/eval_jaxpr/ppermute | solution.py:14
  520.1 8.8 %collective-permute-start.2 = (bf16[2,34,1,64]{3,2,1,0:T(2,128)(2,1)S(1)}, bf16[2,34,1,64]{3,2,1,0:T(2,128)(2,1)S(1)}, u32[]{:S(2)}, u32[]{:S(2)}) collective-permute-start(bf16[2,34,1,64]{3,2,1,0:T(2,128)(2,1)S(1)} %get-tuple-element.181), channel_id=1, source_target_pairs={{4,0},{5,1},{6,2},{7,3}} | collective-permute-start | bytes 26120 | tf_op jit(solution)/shard_map/while/body/eval_jaxpr/ppermute | solution.py:14
  521.4 7.5 %collective-permute-start.3 = (bf16[2,34,1,64]{3,2,1,0:T(2,128)(2,1)S(1)}, bf16[2,34,1,64]{3,2,1,0:T(2,128)(2,1)}, u32[]{:S(2)}, u32[]{:S(2)}) collective-permute-start(bf16[2,34,1,64]{3,2,1,0:T(2,128)(2,1)S(1)} %get-tuple-element.182), channel_id=1, source_target_pairs={{0,4},{1,5},{2,6},{3,7}} | collective-permute-start | bytes 26120 | tf_op jit(solution)/shard_map/while/body/eval_jaxpr/ppermute | solution.py:13
  (28 other events, 32.6 us)
where the time goes:
time: 556 us; the launch traced here: 546 us
  local copies, waits for them, and re-layouts  204 us (37%)
  starting transfers between devices  152 us (27%)
  other arithmetic  114 us (21%)
  matrix products  62 us (11%)
  waiting for transfers between devices  11.4 us (2%)
    concatenate x24, local copies, waits for them, and re-layouts, conv_taps(): patches = jnp.concatenate(tap_list, axis=-1)  127 us
    ppermute x26, starting transfers between devices, edge_swap(): from_prev = lax.ppermute(high_edge, axis_label, down_pairs)  119 us
    concatenate x25, other arithmetic, edge_swap(): return jnp.concatenate([from_prev, tile_arr, from_next], axis=split_dim)  85.5 us
    dot_general x24, matrix products, conv_taps(): jnp.dot(flat_patches, flat_weights, preferred_element_type=jnp.float32)  62 us
    ppermute x26, starting transfers between devices, edge_swap(): from_next = lax.ppermute(low_edge, axis_label, up_pairs)  33.6 us
    slice x12, local copies, waits for them, and re-layouts, conv_taps(): padded[:, row_off:row_off + out_rows, col_off:col_off + out_cols, :]  29.1 us
    dynamic_update_slice x12, other arithmetic, local_run(): final_pair, all_hidden = lax.scan(step_fn, (h_init, c_init), frames_ext)  28.8 us
    while x84, local copies, waits for them, and re-layouts  21.4 us
  transfers between devices with their start and end apart: 52, of which 2 were waited for; matrix products, arithmetic and copies ran while one was open for 26% of the time, Pallas kernels for 0%

commit v1 on v0

v1 whole, which is shorter than its diff:
```python
import functools

import jax
import jax.numpy as jnp
from jax import lax
from jax.experimental import pallas as pl
from jax.experimental.pallas import tpu as pltpu
from jax.sharding import PartitionSpec as P

MESH = pl.DeviceIdType.MESH
F32, BF16 = jnp.float32, jnp.bfloat16

DEPTH = 3
STEPS = 12
BLOCKS = STEPS // DEPTH
PAIRS = 16
OWN = 64
EDGE = 2
HP = -(-DEPTH // 2)
ROWS_ALL = PAIRS + 2 * EDGE
SUBL = 88
FROM_UP, FROM_DOWN, FROM_SIDE, FROM_DUP, FROM_DDOWN = range(5)
MIRROR = {FROM_UP: FROM_DOWN, FROM_DOWN: FROM_UP, FROM_SIDE: FROM_SIDE, FROM_DUP: FROM_DDOWN, FROM_DDOWN: FROM_DUP}


def region(j):
    halo = DEPTH - 1 - j
    extra = -(-halo // 2)
    return EDGE - extra, PAIRS + 2 * extra, 72 if halo else OWN


def kernel(frames, wx_in, wh_in, bias_in, h_in, c_in, h_out, c_out,
           fbuf, xs, hs, cs, xg, lhs, gts, wx, wh, bias, obuf,
           sx_row, sx_col, sx_cor, sh_row, sh_col, sh_cor, sc_row, sc_col, sc_cor,
           rx_row, rx_col, rx_cor, rh_row, rh_col, rh_cor, rc_row, rc_col, rc_cor,
           fsem, osem, ssem, rsem):
    row, col, grp = lax.axis_index("rows"), lax.axis_index("cols"), lax.axis_index("batch")
    n_rows = 4
    side = 1 - col
    has_up, has_down = row > 0, row < n_rows - 1
    peers = {
        FROM_UP: (has_up, row - 1, col),
        FROM_DOWN: (has_down, row + 1, col),
        FROM_SIDE: (None, row, side),
        FROM_DUP: (has_up, row - 1, side),
        FROM_DDOWN: (has_down, row + 1, side),
    }

    def guarded(cond, fn):
        if cond is None:
            fn()
        else:
            pl.when(cond)(fn)

    lane = lax.broadcasted_iota(jnp.int32, (72, 128), 1)
    subl = lax.broadcasted_iota(jnp.int32, (8, 128), 0)
    col_mask = jnp.where((subl + 2 * (1 - col) >= 2) & (subl < 6 + 2 * col), 1.0, 0.0).astype(F32)
    up_mask = jnp.where(has_up, 1.0, 0.0).astype(F32)
    down_mask = jnp.where(has_down, 1.0, 0.0).astype(F32)

    def frame_copy(t, slot):
        return pltpu.make_async_copy(frames.at[t], fbuf.at[slot], fsem.at[slot])

    for j in range(DEPTH):
        frame_copy(j, j).start()

    barrier = pltpu.get_barrier_semaphore()
    for cond, r, c in peers.values():
        guarded(cond, lambda r=r, c=c: pl.semaphore_signal(barrier, inc=1, device_id=(grp, c, r), device_id_type=MESH))

    def ingest(load, dst):
        def body(i, _):
            for u in range(4):
                q = i * 4 + u
                for s in range(2):
                    both = jnp.concatenate([load(s, 2 * q), load(s, 2 * q + 1)], axis=1).astype(F32)
                    dst[q, pl.ds(s, 32, stride=2), :] = both
            return 0
        lax.fori_loop(0, PAIRS // 4, body, 0)

    def wrap_first(ref, q):
        ref[q, 80:88, :] = ref[q, 8:16, :]

    hs[...] = jnp.zeros_like(hs)
    cs[...] = jnp.zeros_like(cs)
    xs[...] = jnp.zeros_like(xs)

    ingest(lambda s, r: h_in[s, r], hs.at[pl.ds(EDGE, PAIRS), pl.ds(8, OWN)])
    ingest(lambda s, r: c_in[s, r], cs.at[pl.ds(1, PAIRS), pl.ds(0, OWN)])
    for q in range(PAIRS):
        wrap_first(hs, EDGE + q)

    strip_at = pl.multiple_of(8 + 56 * (1 - col), 8)
    cstrip_at = pl.multiple_of(56 * (1 - col), 8)

    def pack_bf16(src, s_row, s_col, s_cor):
        for p in range(HP):
            s_row[0, p] = src[EDGE + p, 8:72, :].astype(BF16)
            s_row[1, p] = src[EDGE + PAIRS - HP + p, 8:72, :].astype(BF16)
        two = []
        for i in range(PAIRS // 2):
            two.append(jnp.concatenate([src[EDGE + 2 * i, pl.ds(strip_at, 8), :],
                                        src[EDGE + 2 * i + 1, pl.ds(strip_at, 8), :]], axis=0).astype(BF16))
            s_col[i] = two[-1]
        s_cor[0] = two[0]
        s_cor[1] = two[-1]

    def unpack_side(dst, q, strip):
        strip = strip * col_mask
        dst[q, 72:80, :] = strip
        dst[q, 0:8, :] = strip

    def unpack_bf16(dst, get_row, get_col, get_cor):
        for i in range(PAIRS // 2):
            both = get_col(i).astype(F32)
            unpack_side(dst, EDGE + 2 * i, both[0:8])
            unpack_side(dst, EDGE + 2 * i + 1, both[8:16])

        def rows(which, first):
            for p in range(HP):
                strip = get_row(which, p).astype(F32)
                dst[first + p, 8:72, :] = strip
                dst[first + p, 80:88, :] = strip[0:8]
            both = get_cor(which).astype(F32)
            for p in range(HP):
                at = 2 - HP + p if which == 0 else p
                unpack_side(dst, first + p, both[8 * at:8 * at + 8])

        pl.when(has_up)(lambda: rows(0, EDGE - HP))
        pl.when(has_down)(lambda: rows(1, EDGE + PAIRS))

    def copies(b, kind, sends, recvs):
        s_row, s_col, s_cor = sends
        r_row, r_col, r_cor = recvs
        out = []
        for d, (cond, r, c) in peers.items():
            m = MIRROR[d]
            if d in (FROM_UP, FROM_DOWN):
                src, dst = s_row.at[d], r_row.at[m]
            elif d == FROM_SIDE:
                src, dst = s_col, r_col
            else:
                src, dst = s_cor.at[d - FROM_DUP], r_cor.at[m - FROM_DUP]
            out.append((cond, pltpu.make_async_remote_copy(
                src_ref=src, dst_ref=dst, send_sem=ssem.at[b, kind, d], recv_sem=rsem.at[b, kind, m],
                device_id=(grp, c, r), device_id_type=MESH)))
        return out

    def waits(b, kind, sends, recvs):
        s_row, s_col, s_cor = sends
        r_row, r_col, r_cor = recvs
        out = []
        for d, (cond, r, c) in peers.items():
            if d in (FROM_UP, FROM_DOWN):
                src, dst = s_row.at[d], r_row.at[d]
            elif d == FROM_SIDE:
                src, dst = s_col, r_col
            else:
                src, dst = s_cor.at[d - FROM_DUP], r_cor.at[d - FROM_DUP]
            out.append((cond, pltpu.make_async_remote_copy(
                src_ref=src, dst_ref=dst, send_sem=ssem.at[b, kind, d], recv_sem=rsem.at[b, kind, d],
                device_id=(grp, c, r), device_id_type=MESH)))
        return out

    def bufs(b, kind):
        if kind == 0:
            return ((sx_row.at[b], sx_col.at[b], sx_cor.at[b]), (rx_row.at[b], rx_col.at[b], rx_cor.at[b]))
        if kind == 1:
            return ((sh_row.at[b], sh_col.at[b], sh_cor.at[b]), (rh_row.at[b], rh_col.at[b], rh_cor.at[b]))
        return ((sc_row.at[b], sc_col.at[b], sc_cor.at[b]), (rc_row.at[b], rc_col.at[b], rc_cor.at[b]))

    def send(b, kind):
        for cond, cp in copies(b, kind, *bufs(b, kind)):
            guarded(cond, lambda cp=cp: cp.start())

    def receive(b, kind):
        for cond, cp in waits(b, kind, *bufs(b, kind)):
            guarded(cond, lambda cp=cp: cp.wait_recv())

    def send_state(b):
        pack_bf16(hs, sh_row.at[b], sh_col.at[b], sh_cor.at[b])
        if DEPTH > 1:
            sc_row[b, 0] = cs[1, 0:OWN, :]
            sc_row[b, 1] = cs[PAIRS, 0:OWN, :]
            for q in range(PAIRS):
                sc_col[b, q] = cs[1 + q, pl.ds(cstrip_at, 8), :]
            sc_cor[b, 0] = cs[1, pl.ds(cstrip_at, 8), :]
            sc_cor[b, 1] = cs[PAIRS, pl.ds(cstrip_at, 8), :]
        send(b, 1)
        if DEPTH > 1:
            send(b, 2)

    def receive_state(b):
        receive(b, 1)
        unpack_bf16(hs, lambda w, p: rh_row[b, w, p], lambda i: rh_col[b, i], lambda w: rh_cor[b, w])
        if DEPTH > 1:
            receive(b, 2)
            for q in range(PAIRS):
                cs[1 + q, 64:72, :] = rc_col[b, q]

            def rows(which, at):
                cs[at, 0:OWN, :] = rc_row[b, which]
                cs[at, 64:72, :] = rc_cor[b, which]

            pl.when(has_up)(lambda: rows(0, 0))
            pl.when(has_down)(lambda: rows(1, 1 + PAIRS))

    def send_frames(b):
        for j in range(DEPTH):
            frame_copy(0, j).wait()
            ingest(lambda s, r: fbuf[j, s, r], xs.at[j, pl.ds(EDGE, PAIRS), pl.ds(8, OWN)])
            for q in range(PAIRS):
                wrap_first(xs.at[j], EDGE + q)
            pack_bf16(xs.at[j], sx_row.at[b, :, j], sx_col.at[b, j], sx_cor.at[b, :, j])
        send(b, 0)

        @pl.when(b + 1 < BLOCKS)
        def _():
            for j in range(DEPTH):
                frame_copy((b + 1) * DEPTH + j, j).start()

    def build(src, j):
        first, count, width = region(j)
        low = (lane < 64)[0:width]
        for q in range(0, count, 2):
            for dx in range(3):
                at = pl.ds(6 + 2 * dx, width)
                r = [src[first + q + i, at, :] for i in range(-1, 3)]
                own = jnp.concatenate([r[1], r[2]], axis=0).astype(BF16)
                near = jnp.concatenate([jnp.where(low, r[2], r[0]), jnp.where(low, r[3], r[1])], axis=0).astype(BF16)
                lhs[q * width:(q + 2) * width, dx * 256:dx * 256 + 128] = own
                lhs[q * width:(q + 2) * width, dx * 256 + 128:dx * 256 + 256] = near

    def chunks(j):
        first, count, width = region(j)
        step = 6 if count == 18 else 8
        return [(g, step) for g in range(0, count, step)]

    def conv_x(b):
        receive(b, 0)
        for j in range(DEPTH):
            unpack_bf16(xs.at[j], lambda w, p: rx_row[b, w, j, p], lambda i: rx_col[b, j, i], lambda w: rx_cor[b, w, j])
        for j in range(DEPTH):
            first, count, width = region(j)
            build(xs.at[j], j)
            for g, n in chunks(j):
                rows = pl.ds(g * width, n * width)
                xg[j, rows, :] = jnp.dot(lhs[rows, :], wx[...], preferred_element_type=F32) + bias[...]

    def step(j):
        first, count, width = region(j)
        build(hs, j)
        for g, n in chunks(j):
            rows = pl.ds(g * width, n * width)
            gts[rows, :] = jnp.dot(lhs[rows, :], wh[...], preferred_element_type=F32) + xg[j, rows, :]
            for q in range(g, g + n):
                rows_q = pl.ds(q * width, width)
                gi, gf, go, gg = (gts[rows_q, 128 * i:128 * i + 128] for i in range(4))
                at = first + q
                c_old = cs[at - 1, 0:width, :]
                ti, tf, to = jnp.tanh(0.5 * gi), jnp.tanh(0.5 * gf), jnp.tanh(0.5 * go)
                c_new = 0.5 * ((tf + 1.0) * c_old + (ti + 1.0) * jnp.tanh(gg))
                cs[at - 1, 0:width, :] = c_new
                h_new = 0.5 * (to + 1.0) * jnp.tanh(c_new)
                if at < EDGE:
                    h_new = h_new * up_mask
                if at >= EDGE + PAIRS:
                    h_new = h_new * down_mask
                hs[at, 8:72, :] = h_new[0:OWN]
                hs[at, 80:88, :] = h_new[0:8]
                if width == 72:
                    unpack_side(hs, at, h_new[64:72])

    def out_copy(t, j):
        return pltpu.make_async_copy(obuf.at[j], h_out.at[t], osem.at[j])

    def emit(b, j):
        @pl.when(b > 0)
        def _():
            out_copy(0, j).wait()

        def body(i, _):
            for u in range(4):
                q = i * 4 + u
                for s in range(2):
                    both = hs[EDGE + q, pl.ds(8 + s, 32, stride=2), :].astype(BF16)
                    obuf[j, s, 2 * q] = both[:, 0:64]
                    obuf[j, s, 2 * q + 1] = both[:, 64:128]
            return 0

        lax.fori_loop(0, PAIRS // 4, body, 0)
        out_copy(b * DEPTH + j, j).start()

    def weights(src, dst):
        zero = jnp.zeros((64, 64), BF16)
        for dx in range(3):
            for k, q in enumerate((0, 1, 2, -1)):
                for g in range(4):
                    parts = []
                    for p in range(2):
                        dy = q - p + 1
                        parts.append(src[dy, dx, :, 64 * g:64 * g + 64] if 0 <= dy <= 2 else zero)
                    dst[dx * 256 + k * 64:dx * 256 + k * 64 + 64, 128 * g:128 * g + 128] = jnp.concatenate(parts, axis=1)

    count = 3 + 2 * (has_up & has_down).astype(jnp.int32)
    pl.semaphore_wait(barrier, count)
    send_state(0)
    send_frames(0)
    weights(wx_in, wx)
    weights(wh_in, wh)
    for g in range(4):
        piece = bias_in[:, 64 * g:64 * g + 64]
        bias[:, 128 * g:128 * g + 128] = jnp.concatenate([piece, piece], axis=1)
    conv_x(0)

    def block(b, _):
        @pl.when(b + 1 < BLOCKS)
        def _():
            send_frames(b + 1)

        receive_state(b)
        for j in range(DEPTH):
            step(j)
            emit(b, j)

        @pl.when(b + 1 < BLOCKS)
        def _():
            send_state(b + 1)
            conv_x(b + 1)

        return 0

    lax.fori_loop(0, BLOCKS, block, 0)

    def final(i, _):
        for u in range(4):
            q = i * 4 + u
            for s in range(2):
                both = cs[1 + q, pl.ds(s, 32, stride=2), :]
                c_out[s, 2 * q] = both[:, 0:64]
                c_out[s, 2 * q + 1] = both[:, 64:128]
        return 0

    lax.fori_loop(0, PAIRS // 4, final, 0)
    for j in range(DEPTH):
        out_copy(0, j).wait()

    def drain(b, _):
        for kind in range(3 if DEPTH > 1 else 2):
            for cond, cp in copies(b, kind, *bufs(b, kind)):
                guarded(cond, lambda cp=cp: cp.wait_send())
        return 0

    lax.fori_loop(0, BLOCKS, drain, 0)


def solution(mesh):
    frame_spec = P(None, "batch", "rows", "cols", None)
    state_spec = P("batch", "rows", "cols", None)

    def local_run(frames, w_x, w_h, gate_bias, h_init, c_init):
        vmem = pl.BlockSpec(memory_space=pltpu.VMEM)
        hbm = pl.BlockSpec(memory_space=pl.ANY)
        most = max(region(j)[1] * region(j)[2] for j in range(DEPTH))
        strips = [
            [(BLOCKS, 2, DEPTH, HP, OWN, 128), (BLOCKS, DEPTH, 8, 16, 128), (BLOCKS, 2, DEPTH, 16, 128)],
            [(BLOCKS, 2, HP, OWN, 128), (BLOCKS, 8, 16, 128), (BLOCKS, 2, 16, 128)],
            [(BLOCKS, 2, OWN, 128), (BLOCKS, PAIRS, 8, 128), (BLOCKS, 2, 8, 128)],
        ]
        strip_bufs = [pltpu.VMEM(s, BF16 if k < 2 else F32) for k in range(3) for s in strips[k]]
        return pl.pallas_call(
            kernel,
            out_shape=(jax.ShapeDtypeStruct(frames.shape, BF16), jax.ShapeDtypeStruct(c_init.shape, F32)),
            in_specs=[hbm, vmem, vmem, vmem, vmem, vmem],
            out_specs=(hbm, vmem),
            scratch_shapes=[
                pltpu.VMEM((DEPTH,) + h_init.shape, BF16),
                pltpu.VMEM((DEPTH, ROWS_ALL, SUBL, 128), F32),
                pltpu.VMEM((ROWS_ALL, SUBL, 128), F32),
                pltpu.VMEM((PAIRS + 2, 72, 128), F32),
                pltpu.VMEM((DEPTH, most, 512), F32),
                pltpu.VMEM((most, 768), BF16),
                pltpu.VMEM((most, 512), F32),
                pltpu.VMEM((768, 512), BF16),
                pltpu.VMEM((768, 512), BF16),
                pltpu.VMEM((1, 512), F32),
                pltpu.VMEM((DEPTH,) + h_init.shape, BF16),
                *strip_bufs, *strip_bufs,
                pltpu.SemaphoreType.DMA((DEPTH,)),
                pltpu.SemaphoreType.DMA((DEPTH,)),
                pltpu.SemaphoreType.DMA((BLOCKS, 3, 5)),
                pltpu.SemaphoreType.DMA((BLOCKS, 3, 5)),
            ],
            compiler_params=pltpu.CompilerParams(collective_id=0, has_side_effects=True, vmem_limit_bytes=60 * 2**20),
        )(frames, w_x, w_h, gate_bias.reshape(1, 256), h_init, c_init)

    return jax.shard_map(local_run, mesh=mesh, in_specs=(frame_spec, P(), P(), P(), state_spec, state_spec),
                         out_specs=(frame_spec, state_spec), check_vma=False)
```

time: 556 us -> 63.3 us (0.11); the launches traced: 546 us -> 63.2 us
  local copies, waits for them, and re-layouts: 204 us -> 8.17 us
  starting transfers between devices: 152 us -> 0 us
  other arithmetic: 114 us -> 0 us
  matrix products: 62 us -> 0 us
  Pallas kernels: 0 us -> 54.3 us
  waiting for transfers between devices: 11.4 us -> 0 us
    ppermute x52 -> x0, starting transfers between devices: 152 us -> none  [the longest x26 119 us: edge_swap(): from_prev = lax.ppermute(high_edge, axis_label, down_pairs)]
    concatenate x37 -> x0, local copies, waits for them, and re-layouts: 127 us -> none  [the longest x24 127 us: conv_taps(): patches = jnp.concatenate(tap_list, axis=-1)]
    concatenate x25 -> x0, other arithmetic: 85.5 us -> none  [edge_swap(): return jnp.concatenate([from_prev, tile_arr, from_next], axis=split_dim)]
    dot_general x24 -> x0, matrix products: 62 us -> none  [conv_taps(): jnp.dot(flat_patches, flat_weights, preferred_element_type=jnp.float32)]
    pallas_call x0 -> x1, Pallas kernels: none -> 54.3 us  [local_run(): pl.pallas_call(kernel, out_shape=(jax.ShapeDtypeStruct(frames.shape, BF16...]
    slice x38 -> x0, local copies, waits for them, and re-layouts: 31.6 us -> none  [the longest x12 29.1 us: conv_taps(): padded[:, row_off:row_off + out_rows, col_off:col_off + out_cols, :]]
    dynamic_update_slice x12 -> x0, other arithmetic: 28.8 us -> none  [local_run(): final_pair, all_hidden = lax.scan(step_fn, (h_init, c_init), frames_ext)]
    while x84 -> x0, local copies, waits for them, and re-layouts: 21.4 us -> none
  transfers between devices with their start and end apart: 52 -> 0, of which waited for: 2 -> 0; matrix products, arithmetic and copies ran while one was open for 26% -> 0% of each run, Pallas kernels for 0% -> 0%
where the time goes in v1:
time: 63.3 us; the launch traced here: 63.2 us
  Pallas kernels  54.3 us (86%)
  local copies, waits for them, and re-layouts  8.17 us (13%)
  between operations  0.65 us (1%)
    pallas_call x1, Pallas kernels, local_run(): pl.pallas_call(kernel, out_shape=(jax.ShapeDtypeStruct(frames.shape, BF16...  54.3 us
    unnamed x4, local copies, waits for them, and re-layouts  8.17 us

profile of v1, /device:TPU:0, one launch (start us, length us, event | category | flops | bytes accessed | tf_op | source)
XLA Modules:
  0.0 63.2 jit_solution(6739857952038442577)
XLA Ops:
  0.6 54.3 %shard_map.77 = (bf16[12,2,32,32,64]{4,3,2,1,0:T(8,128)(2,1)}, f32[2,32,32,64]{3,2,1,0:T(8,128)}) custom-call(bf16[12,2,32,32,64]{4,3,2,1,0:T(8,128)(2,1)} %frames.1, bf16[3,3,64,256]{3,2,1,0:T(8,128)(2,1)} %wx_in.1, bf16[3,3,64,256]{3,2,1,0:T(8,128)(2,1)} %wh_in.1, f32[1,256]{1,0:T(1,128)} %bitcast.1, bf16[2,32,32,64]{3,2,1,0:T(8,128)(2,1)} %h_in.1, ...), custom_call_target="tpu_custom_call" | custom-call | tf_op jit(solution)/shard_map/pallas_call | solution.py:371
  55.0 0.0 copy-start
  55.0 7.2 %copy.10 = bf16[12,2,32,32,64]{4,3,2,1,0:T(8,128)(2,1)} copy(bf16[12,2,32,32,64]{4,3,2,1,0:T(8,128)(2,1)} %get-tuple-element.4) | data formatting | bytes 6291456
  62.2 0.0 copy-done
  62.2 1.0 %copy.11 = f32[2,32,32,64]{3,2,1,0:T(8,128)} copy(f32[2,32,32,64]{3,2,1,0:T(8,128)S(1)} %copy-done) | data formatting | bytes 1048576
Async XLA Ops:
  55.0 7.2 %copy-start = (f32[2,32,32,64]{3,2,1,0:T(8,128)S(1)}, f32[2,32,32,64]{3,2,1,0:T(8,128)}, u32[]{:S(2)}) copy-start(f32[2,32,32,64]{3,2,1,0:T(8,128)} %get-tuple-element.5) | copy-start | bytes 1572868

commit v2 on v1

--- a/solution.py
+++ b/solution.py
@@ -92,6 +92,8 @@
 
     strip_at = pl.multiple_of(8 + 56 * (1 - col), 8)
     cstrip_at = pl.multiple_of(56 * (1 - col), 8)
+    cstrip_from = pl.multiple_of(60 * (1 - col), 4)
+    cstrip_to = pl.multiple_of(64 + 4 * col, 4)
 
     def pack_bf16(src, s_row, s_col, s_cor):
         for p in range(HP):
@@ -163,9 +165,10 @@
         return out
 
     def bufs(b, kind):
-        if kind == 0:
-            return ((sx_row.at[b], sx_col.at[b], sx_cor.at[b]), (rx_row.at[b], rx_col.at[b], rx_cor.at[b]))
-        if kind == 1:
+        if kind < DEPTH:
+            return ((sx_row.at[b, kind], sx_col.at[b, kind], sx_cor.at[b, kind]),
+                    (rx_row.at[b, kind], rx_col.at[b, kind], rx_cor.at[b, kind]))
+        if kind == DEPTH:
             return ((sh_row.at[b], sh_col.at[b], sh_cor.at[b]), (rh_row.at[b], rh_col.at[b], rh_cor.at[b]))
         return ((sc_row.at[b], sc_col.at[b], sc_cor.at[b]), (rc_row.at[b], rc_col.at[b], rc_cor.at[b]))
 
@@ -183,20 +186,20 @@
             sc_row[b, 0] = cs[1, 0:OWN, :]
             sc_row[b, 1] = cs[PAIRS, 0:OWN, :]
             for q in range(PAIRS):
-                sc_col[b, q] = cs[1 + q, pl.ds(cstrip_at, 8), :]
+                sc_col[b, q // 2, 4 * (q % 2):4 * (q % 2) + 4] = cs[1 + q, pl.ds(cstrip_from, 4), :]
             sc_cor[b, 0] = cs[1, pl.ds(cstrip_at, 8), :]
             sc_cor[b, 1] = cs[PAIRS, pl.ds(cstrip_at, 8), :]
-        send(b, 1)
+        send(b, DEPTH)
         if DEPTH > 1:
-            send(b, 2)
+            send(b, DEPTH + 1)
 
     def receive_state(b):
-        receive(b, 1)
+        receive(b, DEPTH)
         unpack_bf16(hs, lambda w, p: rh_row[b, w, p], lambda i: rh_col[b, i], lambda w: rh_cor[b, w])
         if DEPTH > 1:
-            receive(b, 2)
+            receive(b, DEPTH + 1)
             for q in range(PAIRS):
-                cs[1 + q, 64:72, :] = rc_col[b, q]
+                cs[1 + q, pl.ds(cstrip_to, 4), :] = rc_col[b, q // 2, 4 * (q % 2):4 * (q % 2) + 4]
 
             def rows(which, at):
                 cs[at, 0:OWN, :] = rc_row[b, which]
@@ -205,91 +208,110 @@
             pl.when(has_up)(lambda: rows(0, 0))
             pl.when(has_down)(lambda: rows(1, 1 + PAIRS))
 
-    def send_frames(b):
-        for j in range(DEPTH):
-            frame_copy(0, j).wait()
-            ingest(lambda s, r: fbuf[j, s, r], xs.at[j, pl.ds(EDGE, PAIRS), pl.ds(8, OWN)])
-            for q in range(PAIRS):
-                wrap_first(xs.at[j], EDGE + q)
-            pack_bf16(xs.at[j], sx_row.at[b, :, j], sx_col.at[b, j], sx_cor.at[b, :, j])
-        send(b, 0)
-
-        @pl.when(b + 1 < BLOCKS)
-        def _():
-            for j in range(DEPTH):
-                frame_copy((b + 1) * DEPTH + j, j).start()
-
-    def build(src, j):
+    def take_frame(b, j, pairs):
+        for q in pairs:
+            for s in range(2):
+                both = jnp.concatenate([fbuf[j, s, 2 * q], fbuf[j, s, 2 * q + 1]], axis=1).astype(F32)
+                xs[j, EDGE + q, pl.ds(8 + s, 32, stride=2), :] = both
+            wrap_first(xs.at[j], EDGE + q)
+
+    def pack_frame(b, j):
+        pack_bf16(xs.at[j], sx_row.at[b, j], sx_col.at[b, j], sx_cor.at[b, j])
+
+    def tasks(j):
         first, count, width = region(j)
+        n = 6 if count == 18 else 8
+        return [(j, first + g, n, width, g * width) for g in range(0, count, n)]
+
+    def build(src, slot, task):
+        _, first, n, width, _ = task
         low = (lane < 64)[0:width]
-        for q in range(0, count, 2):
+        for q in range(0, n, 2):
             for dx in range(3):
                 at = pl.ds(6 + 2 * dx, width)
                 r = [src[first + q + i, at, :] for i in range(-1, 3)]
                 own = jnp.concatenate([r[1], r[2]], axis=0).astype(BF16)
                 near = jnp.concatenate([jnp.where(low, r[2], r[0]), jnp.where(low, r[3], r[1])], axis=0).astype(BF16)
-                lhs[q * width:(q + 2) * width, dx * 256:dx * 256 + 128] = own
-                lhs[q * width:(q + 2) * width, dx * 256 + 128:dx * 256 + 256] = near
-
-    def chunks(j):
-        first, count, width = region(j)
-        step = 6 if count == 18 else 8
-        return [(g, step) for g in range(0, count, step)]
-
-    def conv_x(b):
-        receive(b, 0)
+                lhs[slot, q * width:(q + 2) * width, dx * 256:dx * 256 + 128] = own
+                lhs[slot, q * width:(q + 2) * width, dx * 256 + 128:dx * 256 + 256] = near
+
+    def product(slot, task, w):
+        _, _, n, width, _ = task
+        return jnp.dot(lhs[slot, 0:n * width, :], w[...], preferred_element_type=F32)
+
+    def conv_x(b, following):
         for j in range(DEPTH):
-            unpack_bf16(xs.at[j], lambda w, p: rx_row[b, w, j, p], lambda i: rx_col[b, j, i], lambda w: rx_cor[b, w, j])
+            receive(b, j)
         for j in range(DEPTH):
-            first, count, width = region(j)
-            build(xs.at[j], j)
-            for g, n in chunks(j):
-                rows = pl.ds(g * width, n * width)
-                xg[j, rows, :] = jnp.dot(lhs[rows, :], wx[...], preferred_element_type=F32) + bias[...]
-
-    def step(j):
-        first, count, width = region(j)
-        build(hs, j)
-        for g, n in chunks(j):
-            rows = pl.ds(g * width, n * width)
-            gts[rows, :] = jnp.dot(lhs[rows, :], wh[...], preferred_element_type=F32) + xg[j, rows, :]
-            for q in range(g, g + n):
-                rows_q = pl.ds(q * width, width)
-                gi, gf, go, gg = (gts[rows_q, 128 * i:128 * i + 128] for i in range(4))
-                at = first + q
-                c_old = cs[at - 1, 0:width, :]
-                ti, tf, to = jnp.tanh(0.5 * gi), jnp.tanh(0.5 * gf), jnp.tanh(0.5 * go)
-                c_new = 0.5 * ((tf + 1.0) * c_old + (ti + 1.0) * jnp.tanh(gg))
-                cs[at - 1, 0:width, :] = c_new
-                h_new = 0.5 * (to + 1.0) * jnp.tanh(c_new)
-                if at < EDGE:
-                    h_new = h_new * up_mask
-                if at >= EDGE + PAIRS:
-                    h_new = h_new * down_mask
-                hs[at, 8:72, :] = h_new[0:OWN]
-                hs[at, 80:88, :] = h_new[0:8]
-                if width == 72:
-                    unpack_side(hs, at, h_new[64:72])
+            unpack_bf16(xs.at[j], lambda w, p: rx_row[b, j, w, p], lambda i: rx_col[b, j, i], lambda w: rx_cor[b, j, w])
+
+        @pl.when(following < BLOCKS)
+        def _():
+            for j in range(DEPTH):
+                frame_copy(0, j).wait()
+
+        todo = [t for j in range(DEPTH) for t in tasks(j)]
+        build(xs.at[0], 0, todo[0])
+        for i, task in enumerate(todo):
+            if i + 1 < len(todo):
+                build(xs.at[todo[i + 1][0]], (i + 1) % 2, todo[i + 1])
+            j, _, n, width, at = task
+            xg[j, at:at + n * width, :] = product(i % 2, task, wx) + bias[...]
+            if i + 1 == len(todo) or todo[i + 1][0] != j:
+                take_frame(following, j, range(PAIRS))
+                pack_frame(following, j)
+
+        @pl.when(following < BLOCKS)
+        def _():
+            for j in range(DEPTH):
+                send(following, j)
+
+        @pl.when(following + 1 < BLOCKS)
+        def _():
+            for j in range(DEPTH):
+                frame_copy((following + 1) * DEPTH + j, j).start()
+
+    def cells(slot, task):
+        j, first, n, width, base = task
+        gts[slot, 0:n * width, :] = product(slot, task, wh) + xg[j, base:base + n * width, :]
+        for q in range(n):
+            rows_q = pl.ds(q * width, width)
+            gi, gf, go, gg = (gts[slot, rows_q, 128 * i:128 * i + 128] for i in range(4))
+            at = first + q
+            c_old = cs[at - 1, 0:width, :]
+            ti, tf, to = jnp.tanh(0.5 * gi), jnp.tanh(0.5 * gf), jnp.tanh(0.5 * go)
+            c_new = 0.5 * ((tf + 1.0) * c_old + (ti + 1.0) * jnp.tanh(gg))
+            cs[at - 1, 0:width, :] = c_new
+            h_new = 0.5 * (to + 1.0) * jnp.tanh(c_new)
+            if at < EDGE:
+                h_new = h_new * up_mask
+            if at >= EDGE + PAIRS:
+                h_new = h_new * down_mask
+            hs[at, 8:72, :] = h_new[0:OWN]
+            hs[at, 80:88, :] = h_new[0:8]
+            if width == 72:
+                unpack_side(hs, at, h_new[64:72])
+            if EDGE <= at < EDGE + PAIRS:
+                for s in range(2):
+                    obuf[j, s, at - EDGE] = hs[at, pl.ds(8 + s, 32, stride=2), :].astype(BF16)
 
     def out_copy(t, j):
         return pltpu.make_async_copy(obuf.at[j], h_out.at[t], osem.at[j])
 
-    def emit(b, j):
+    def steps(b):
         @pl.when(b > 0)
         def _():
-            out_copy(0, j).wait()
-
-        def body(i, _):
-            for u in range(4):
-                q = i * 4 + u
-                for s in range(2):
-                    both = hs[EDGE + q, pl.ds(8 + s, 32, stride=2), :].astype(BF16)
-                    obuf[j, s, 2 * q] = both[:, 0:64]
-                    obuf[j, s, 2 * q + 1] = both[:, 64:128]
-            return 0
-
-        lax.fori_loop(0, PAIRS // 4, body, 0)
-        out_copy(b * DEPTH + j, j).start()
+            for j in range(DEPTH):
+                out_copy(0, j).wait()
+
+        todo = [t for j in range(DEPTH) for t in tasks(j)]
+        build(hs, 0, todo[0])
+        for i, task in enumerate(todo):
+            if i + 1 < len(todo):
+                build(hs, (i + 1) % 2, todo[i + 1])
+            cells(i % 2, task)
+            if i + 1 == len(todo) or todo[i + 1][0] != task[0]:
+                out_copy(b * DEPTH + task[0], task[0]).start()
 
     def weights(src, dst):
         zero = jnp.zeros((64, 64), BF16)
@@ -302,56 +324,66 @@
                         parts.append(src[dy, dx, :, 64 * g:64 * g + 64] if 0 <= dy <= 2 else zero)
                     dst[dx * 256 + k * 64:dx * 256 + k * 64 + 64, 128 * g:128 * g + 128] = jnp.concatenate(parts, axis=1)
 
+    for j in range(DEPTH):
+        frame_copy(0, j).wait()
+        ingest(lambda s, r: fbuf[j, s, r], xs.at[j, pl.ds(EDGE, PAIRS), pl.ds(8, OWN)])
+        for q in range(PAIRS):
+            wrap_first(xs.at[j], EDGE + q)
+        pack_frame(0, j)
+    for j in range(DEPTH):
+        frame_copy(DEPTH + j, j).start()
     count = 3 + 2 * (has_up & has_down).astype(jnp.int32)
     pl.semaphore_wait(barrier, count)
+    for j in range(DEPTH):
+        send(0, j)
     send_state(0)
-    send_frames(0)
     weights(wx_in, wx)
     weights(wh_in, wh)
     for g in range(4):
         piece = bias_in[:, 64 * g:64 * g + 64]
         bias[:, 128 * g:128 * g + 128] = jnp.concatenate([piece, piece], axis=1)
-    conv_x(0)
+    conv_x(0, 1)
 
     def block(b, _):
-        @pl.when(b + 1 < BLOCKS)
-        def _():
-            send_frames(b + 1)
-
         receive_state(b)
-        for j in range(DEPTH):
-            step(j)
-            emit(b, j)
-
-        @pl.when(b + 1 < BLOCKS)
-        def _():
-            send_state(b + 1)
-            conv_x(b + 1)
-
+        steps(b)
+        send_state(b + 1)
+        conv_x(b + 1, b + 2)
         return 0
 
-    lax.fori_loop(0, BLOCKS, block, 0)
-
-    def final(i, _):
-        for u in range(4):
-            q = i * 4 + u
-            for s in range(2):
-                both = cs[1 + q, pl.ds(s, 32, stride=2), :]
-                c_out[s, 2 * q] = both[:, 0:64]
-                c_out[s, 2 * q + 1] = both[:, 64:128]
-        return 0
-
-    lax.fori_loop(0, PAIRS // 4, final, 0)
+    lax.fori_loop(0, BLOCKS - 1, block, 0)
+    receive_state(BLOCKS - 1)
+    steps(BLOCKS - 1)
+
+    for q in range(PAIRS):
+        for s in range(2):
+            c_out[s, q] = cs[1 + q, pl.ds(s, 32, stride=2), :]
     for j in range(DEPTH):
         out_copy(0, j).wait()
 
     def drain(b, _):
-        for kind in range(3 if DEPTH > 1 else 2):
+        for kind in range(DEPTH + 2 if DEPTH > 1 else DEPTH + 1):
             for cond, cp in copies(b, kind, *bufs(b, kind)):
                 guarded(cond, lambda cp=cp: cp.wait_send())
         return 0
 
     lax.fori_loop(0, BLOCKS, drain, 0)
+
+
+def expand(h_ref, c_ref, h_out, c_out):
+    for s in range(2):
+        for q in range(PAIRS):
+            both = h_ref[0, s, q]
+            h_out[0, s, 2 * q] = both[:, 0:64]
+            h_out[0, s, 2 * q + 1] = both[:, 64:128]
+
+    @pl.when(pl.program_id(0) == 0)
+    def _():
+        for s in range(2):
+            for q in range(PAIRS):
+                both = c_ref[s, q]
+                c_out[s, 2 * q] = both[:, 0:64]
+                c_out[s, 2 * q + 1] = both[:, 64:128]
 
 
 def solution(mesh):
@@ -363,14 +395,17 @@
         hbm = pl.BlockSpec(memory_space=pl.ANY)
         most = max(region(j)[1] * region(j)[2] for j in range(DEPTH))
         strips = [
-            [(BLOCKS, 2, DEPTH, HP, OWN, 128), (BLOCKS, DEPTH, 8, 16, 128), (BLOCKS, 2, DEPTH, 16, 128)],
+            [(BLOCKS, DEPTH, 2, HP, OWN, 128), (BLOCKS, DEPTH, 8, 16, 128), (BLOCKS, DEPTH, 2, 16, 128)],
             [(BLOCKS, 2, HP, OWN, 128), (BLOCKS, 8, 16, 128), (BLOCKS, 2, 16, 128)],
-            [(BLOCKS, 2, OWN, 128), (BLOCKS, PAIRS, 8, 128), (BLOCKS, 2, 8, 128)],
+            [(BLOCKS, 2, OWN, 128), (BLOCKS, PAIRS // 2, 8, 128), (BLOCKS, 2, 8, 128)],
         ]
-        strip_bufs = [pltpu.VMEM(s, BF16 if k < 2 else F32) for k in range(3) for s in strips[k]]
-        return pl.pallas_call(
+        recv_bufs = [pltpu.VMEM(s, BF16 if k < 2 else F32) for k in range(3) for s in strips[k]]
+        strips[0] = [(s[0] + 1,) + s[1:] for s in strips[0]]
+        send_bufs = [pltpu.VMEM(s, BF16 if k < 2 else F32) for k in range(3) for s in strips[k]]
+        h_pairs, c_pairs = pl.pallas_call(
             kernel,
-            out_shape=(jax.ShapeDtypeStruct(frames.shape, BF16), jax.ShapeDtypeStruct(c_init.shape, F32)),
+            out_shape=(jax.ShapeDtypeStruct((STEPS, 2, PAIRS, 32, 128), BF16),
+                       jax.ShapeDtypeStruct((2, PAIRS, 32, 128), F32)),
             in_specs=[hbm, vmem, vmem, vmem, vmem, vmem],
             out_specs=(hbm, vmem),
             scratch_shapes=[
@@ -379,20 +414,29 @@
                 pltpu.VMEM((ROWS_ALL, SUBL, 128), F32),
                 pltpu.VMEM((PAIRS + 2, 72, 128), F32),
                 pltpu.VMEM((DEPTH, most, 512), F32),
-                pltpu.VMEM((most, 768), BF16),
-                pltpu.VMEM((most, 512), F32),
+                pltpu.VMEM((2, 512, 768), BF16),
+                pltpu.VMEM((2, 512, 512), F32),
                 pltpu.VMEM((768, 512), BF16),
                 pltpu.VMEM((768, 512), BF16),
                 pltpu.VMEM((1, 512), F32),
-                pltpu.VMEM((DEPTH,) + h_init.shape, BF16),
-                *strip_bufs, *strip_bufs,
+                pltpu.VMEM((DEPTH, 2, PAIRS, 32, 128), BF16),
+                *send_bufs, *recv_bufs,
                 pltpu.SemaphoreType.DMA((DEPTH,)),
                 pltpu.SemaphoreType.DMA((DEPTH,)),
-                pltpu.SemaphoreType.DMA((BLOCKS, 3, 5)),
-                pltpu.SemaphoreType.DMA((BLOCKS, 3, 5)),
+                pltpu.SemaphoreType.DMA((BLOCKS, DEPTH + 2, 5)),
+                pltpu.SemaphoreType.DMA((BLOCKS, DEPTH + 2, 5)),
             ],
             compiler_params=pltpu.CompilerParams(collective_id=0, has_side_effects=True, vmem_limit_bytes=60 * 2**20),
         )(frames, w_x, w_h, gate_bias.reshape(1, 256), h_init, c_init)
+        return pl.pallas_call(
+            expand,
+            grid=(STEPS,),
+            out_shape=(jax.ShapeDtypeStruct(frames.shape, BF16), jax.ShapeDtypeStruct(c_init.shape, F32)),
+            in_specs=[pl.BlockSpec((1, 2, PAIRS, 32, 128), lambda t: (t, 0, 0, 0, 0)),
+                      pl.BlockSpec((2, PAIRS, 32, 128), lambda t: (0, 0, 0, 0))],
+            out_specs=(pl.BlockSpec((1,) + frames.shape[1:], lambda t: (t, 0, 0, 0, 0)),
+                       pl.BlockSpec(c_init.shape, lambda t: (0, 0, 0, 0))),
+        )(h_pairs, c_pairs)
 
     return jax.shard_map(local_run, mesh=mesh, in_specs=(frame_spec, P(), P(), P(), state_spec, state_spec),
                          out_specs=(frame_spec, state_spec), check_vma=False)

time: 63.3 us -> 56.7 us (0.90)
  local copies, waits for them, and re-layouts: 8.17 us -> 0 us
  Pallas kernels: 54.3 us -> 55.7 us
    unnamed x4 -> x0, local copies, waits for them, and re-layouts: 8.17 us -> none
    pallas_call x1 -> x2, Pallas kernels: 54.3 us -> 55.7 us  [the longest x1 45.6 us: local_run(): pl.pallas_call(kernel, out_shape=(jax.ShapeDtypeStruct((STEPS, 2, PAIRS,...]
where the time goes in v2:
time: 56.7 us; the launch traced here: 56.3 us
  Pallas kernels  55.7 us (98%)
  between operations  0.64 us (1%)
    pallas_call x1, Pallas kernels, local_run(): pl.pallas_call(kernel, out_shape=(jax.ShapeDtypeStruct((STEPS, 2, PAIRS,...  45.6 us
    pallas_call x1, Pallas kernels, local_run(): pl.pallas_call(expand, grid=(STEPS,), out_shape=(jax.ShapeDtypeStruct(fra...  10.1 us

profile of v2, /device:TPU:0, one launch (start us, length us, event | category | flops | bytes accessed | tf_op | source)
XLA Modules:
  0.0 56.3 jit_solution(14952295406109787419)
XLA Ops:
  0.6 45.6 %shard_map.77 = (bf16[12,2,16,32,128]{4,3,2,1,0:T(8,128)(2,1)}, f32[2,16,32,128]{3,2,1,0:T(8,128)}) custom-call(bf16[12,2,32,32,64]{4,3,2,1,0:T(8,128)(2,1)} %frames.1, bf16[3,3,64,256]{3,2,1,0:T(8,128)(2,1)} %wx_in.1, bf16[3,3,64,256]{3,2,1,0:T(8,128)(2,1)} %wh_in.1, f32[1,256]{1,0:T(1,128)} %bitcast.1, bf16[2,32,32,64]{3,2,1,0:T(8,128)(2,1)} %h_in.1, ...), custom_call_target="tpu_custom_call" | custom-call | tf_op jit(solution)/shard_map/pallas_call | solution.py:405
  46.2 10.1 %shard_map.78 = (bf16[12,2,32,32,64]{4,3,2,1,0:T(8,128)(2,1)}, f32[2,32,32,64]{3,2,1,0:T(8,128)}) custom-call(bf16[12,2,16,32,128]{4,3,2,1,0:T(8,128)(2,1)} %get-tuple-element.4.h_ref, f32[2,16,32,128]{3,2,1,0:T(8,128)} %get-tuple-element.5.c_ref), custom_call_target="tpu_custom_call" | custom-call | tf_op jit(solution)/shard_map/pallas_call | solution.py:431

commit v3 on v2

v3 whole, which is shorter than its diff:
```python
import functools

import jax
import jax.numpy as jnp
from jax import lax
from jax.experimental import pallas as pl
from jax.experimental.pallas import tpu as pltpu
from jax.sharding import PartitionSpec as P

MESH = pl.DeviceIdType.MESH
F32, BF16 = jnp.float32, jnp.bfloat16

DEPTH = 3
STEPS = 12
BLOCKS = STEPS // DEPTH
PAIRS = 16
OWN = 64
EDGE = 2
HP = -(-DEPTH // 2)
ROWS_ALL = PAIRS + 2 * EDGE
SUBL = 88
FROM_UP, FROM_DOWN, FROM_SIDE_A, FROM_SIDE_B, FROM_DUP, FROM_DDOWN = range(6)
MIRROR = (FROM_DOWN, FROM_UP, FROM_SIDE_A, FROM_SIDE_B, FROM_DDOWN, FROM_DUP)


def region(j):
    halo = DEPTH - 1 - j
    extra = -(-halo // 2)
    return EDGE - extra, PAIRS + 2 * extra, 72 if halo else OWN


def kernel(frames, wx_hbm, wh_hbm, bias_hbm, h_hbm, c_hbm, h_out, c_out,
           fbuf, wx_in, wh_in, bias_in, h_in, c_in, xs, hs, cs, xg, lhs, gts, wx, wh, bias,
           sx_row, sx_col, sx_cor, sh_row, sh_col, sh_cor, sc_row, sc_col, sc_cor,
           rx_row, rx_col, rx_cor, rh_row, rh_col, rh_cor, rc_row, rc_col, rc_cor,
           fsem, isem, ssem, rsem):
    row, col, grp = lax.axis_index("rows"), lax.axis_index("cols"), lax.axis_index("batch")
    n_rows = 4
    side = 1 - col
    has_up, has_down = row > 0, row < n_rows - 1
    peers = {
        FROM_UP: (has_up, row - 1, col),
        FROM_DOWN: (has_down, row + 1, col),
        FROM_SIDE_A: (None, row, side),
        FROM_SIDE_B: (None, row, side),
        FROM_DUP: (has_up, row - 1, side),
        FROM_DDOWN: (has_down, row + 1, side),
    }

    def guarded(cond, fn):
        if cond is None:
            fn()
        else:
            pl.when(cond)(fn)

    lane = lax.broadcasted_iota(jnp.int32, (72, 128), 1)
    subl = lax.broadcasted_iota(jnp.int32, (8, 128), 0)
    col_mask = jnp.where((subl + 2 * (1 - col) >= 2) & (subl < 6 + 2 * col), 1.0, 0.0).astype(F32)
    up_mask = jnp.where(has_up, 1.0, 0.0).astype(F32)
    down_mask = jnp.where(has_down, 1.0, 0.0).astype(F32)

    def frame_copy(t, slot):
        return pltpu.make_async_copy(frames.at[t], fbuf.at[slot], fsem.at[slot])

    for j in range(DEPTH):
        frame_copy(j, j).start()

    inputs = [pltpu.make_async_copy(src, dst, isem.at[i]) for i, (src, dst) in enumerate(
        ((h_hbm, h_in), (c_hbm, c_in), (wx_hbm, wx_in), (wh_hbm, wh_in), (bias_hbm, bias_in)))]
    for cp in inputs:
        cp.start()

    barrier = pltpu.get_barrier_semaphore()
    for d, (cond, r, c) in peers.items():
        if d == FROM_SIDE_B:
            continue
        guarded(cond, lambda r=r, c=c: pl.semaphore_signal(barrier, inc=1, device_id=(grp, c, r), device_id_type=MESH))

    def ingest(load, dst):
        def body(i, _):
            for u in range(4):
                q = i * 4 + u
                for s in range(2):
                    both = jnp.concatenate([load(s, 2 * q), load(s, 2 * q + 1)], axis=1).astype(F32)
                    dst[q, pl.ds(s, 32, stride=2), :] = both
            return 0
        lax.fori_loop(0, PAIRS // 4, body, 0)

    def wrap_first(ref, q):
        ref[q, 80:88, :] = ref[q, 8:16, :]

    nil = jnp.zeros((SUBL, 128), F32)
    for q in (0, 1, ROWS_ALL - 2, ROWS_ALL - 1):
        hs[q] = nil
        for j in range(DEPTH):
            xs[j, q] = nil
    for q in (0, PAIRS + 1):
        cs[q] = nil[0:72]
    for q in range(PAIRS):
        cs[1 + q, 64:72, :] = nil[0:8]

    strip_at = pl.multiple_of(8 + 56 * (1 - col), 8)
    cstrip_at = pl.multiple_of(56 * (1 - col), 8)
    cstrip_from = pl.multiple_of(60 * (1 - col), 4)
    cstrip_to = pl.multiple_of(64 + 4 * col, 4)

    def pack_rows(src, s_row):
        for p in range(HP):
            s_row[0, p] = src[EDGE + p, 8:72, :].astype(BF16)
            s_row[1, p] = src[EDGE + PAIRS - HP + p, 8:72, :].astype(BF16)

    def pack_cols(src, s_col, s_cor, part):
        for i in range(4 * part, 4 * part + 4):
            two = jnp.concatenate([src[EDGE + 2 * i, pl.ds(strip_at, 8), :],
                                   src[EDGE + 2 * i + 1, pl.ds(strip_at, 8), :]], axis=0).astype(BF16)
            s_col[i] = two
            if i == 0:
                s_cor[0] = two
            if i == PAIRS // 2 - 1:
                s_cor[1] = two

    def unpack_side(dst, q, strip):
        strip = strip * col_mask
        dst[q, 72:80, :] = strip
        dst[q, 0:8, :] = strip

    def unpack_bf16(dst, get_row, get_col, get_cor):
        for i in range(PAIRS // 2):
            both = get_col(i).astype(F32)
            unpack_side(dst, EDGE + 2 * i, both[0:8])
            unpack_side(dst, EDGE + 2 * i + 1, both[8:16])

        def rows(which, first):
            for p in range(HP):
                strip = get_row(which, p).astype(F32)
                dst[first + p, 8:72, :] = strip
                dst[first + p, 80:88, :] = strip[0:8]
            both = get_cor(which).astype(F32)
            for p in range(HP):
                at = 2 - HP + p if which == 0 else p
                unpack_side(dst, first + p, both[8 * at:8 * at + 8])

        pl.when(has_up)(lambda: rows(0, EDGE - HP))
        pl.when(has_down)(lambda: rows(1, EDGE + PAIRS))

    def copies(b, kind, dirs, arriving=False):
        (s_row, s_col, s_cor), (r_row, r_col, r_cor) = bufs(b, kind)
        out = {}
        for d in dirs:
            cond, r, c = peers[d]
            m = d if arriving else MIRROR[d]
            if d in (FROM_UP, FROM_DOWN):
                src, dst = s_row.at[d], r_row.at[m]
            elif d in (FROM_SIDE_A, FROM_SIDE_B):
                half = pl.ds(4 * (d - FROM_SIDE_A), 4)
                src, dst = s_col.at[half], r_col.at[half]
            else:
                src, dst = s_cor.at[d - FROM_DUP], r_cor.at[m - FROM_DUP]
            out[d] = (cond, pltpu.make_async_remote_copy(
                src_ref=src, dst_ref=dst, send_sem=ssem.at[b, kind, d], recv_sem=rsem.at[b, kind, m],
                device_id=(grp, c, r), device_id_type=MESH))
        return out

    def bufs(b, kind):
        if kind < DEPTH:
            return ((sx_row.at[b, kind], sx_col.at[b, kind], sx_cor.at[b, kind]),
                    (rx_row.at[b, kind], rx_col.at[b, kind], rx_cor.at[b, kind]))
        if kind == DEPTH:
            return ((sh_row.at[b], sh_col.at[b], sh_cor.at[b]), (rh_row.at[b], rh_col.at[b], rh_cor.at[b]))
        return ((sc_row.at[b], sc_col.at[b], sc_cor.at[b]), (rc_row.at[b], rc_col.at[b], rc_cor.at[b]))

    OTHERS = (FROM_UP, FROM_DOWN, FROM_DUP, FROM_DDOWN)

    def send(b, kind, dirs):
        for cond, cp in copies(b, kind, dirs).values():
            guarded(cond, lambda cp=cp: cp.start())

    def receive(b, kind):
        for cond, cp in copies(b, kind, peers, arriving=True).values():
            guarded(cond, lambda cp=cp: cp.wait_recv())

    def send_state_cols(b, part):
        pack_cols(hs, sh_col.at[b], sh_cor.at[b], part)
        for q in range(8 * part, 8 * part + 8):
            sc_col[b, q // 2, 4 * (q % 2):4 * (q % 2) + 4] = cs[1 + q, pl.ds(cstrip_from, 4), :]
        for kind in (DEPTH, DEPTH + 1):
            send(b, kind, (FROM_SIDE_A + part,))

    def send_state_rest(b):
        pack_rows(hs, sh_row.at[b])
        sc_row[b, 0] = cs[1, 0:OWN, :]
        sc_row[b, 1] = cs[PAIRS, 0:OWN, :]
        sc_cor[b, 0] = cs[1, pl.ds(cstrip_at, 8), :]
        sc_cor[b, 1] = cs[PAIRS, pl.ds(cstrip_at, 8), :]
        for kind in (DEPTH, DEPTH + 1):
            send(b, kind, OTHERS)

    def receive_state(b):
        receive(b, DEPTH)
        unpack_bf16(hs, lambda w, p: rh_row[b, w, p], lambda i: rh_col[b, i], lambda w: rh_cor[b, w])
        if DEPTH > 1:
            receive(b, DEPTH + 1)
            for q in range(PAIRS):
                cs[1 + q, pl.ds(cstrip_to, 4), :] = rc_col[b, q // 2, 4 * (q % 2):4 * (q % 2) + 4]

            def rows(which, at):
                cs[at, 0:OWN, :] = rc_row[b, which]
                cs[at, 64:72, :] = rc_cor[b, which]

            pl.when(has_up)(lambda: rows(0, 0))
            pl.when(has_down)(lambda: rows(1, 1 + PAIRS))

    def take_frame(b, j, pairs):
        for q in pairs:
            for s in range(2):
                both = jnp.concatenate([fbuf[j, s, 2 * q], fbuf[j, s, 2 * q + 1]], axis=1).astype(F32)
                xs[j, EDGE + q, pl.ds(8 + s, 32, stride=2), :] = both
            wrap_first(xs.at[j], EDGE + q)

    def pack_frame(b, j):
        pack_rows(xs.at[j], sx_row.at[b, j])
        for part in range(2):
            pack_cols(xs.at[j], sx_col.at[b, j], sx_cor.at[b, j], part)

    def tasks(j):
        first, count, width = region(j)
        n = 6 if count == 18 else 8
        return [(j, first + g, n, width, g * width) for g in range(0, count, n)]

    def build(src, slot, task):
        _, first, n, width, _ = task
        low = (lane < 64)[0:width]
        for q in range(0, n, 2):
            for dx in range(3):
                at = pl.ds(6 + 2 * dx, width)
                r = [src[first + q + i, at, :] for i in range(-1, 3)]
                own = jnp.concatenate([r[1], r[2]], axis=0).astype(BF16)
                near = jnp.concatenate([jnp.where(low, r[2], r[0]), jnp.where(low, r[3], r[1])], axis=0).astype(BF16)
                lhs[slot, q * width:(q + 2) * width, dx * 256:dx * 256 + 128] = own
                lhs[slot, q * width:(q + 2) * width, dx * 256 + 128:dx * 256 + 256] = near

    def product(slot, task, w):
        _, _, n, width, _ = task
        return jnp.dot(lhs[slot, 0:n * width, :], w[...], preferred_element_type=F32)

    def conv_x(b, following, early=False):
        def arrive(j):
            receive(b, j)
            unpack_bf16(xs.at[j], lambda w, p: rx_row[b, j, w, p], lambda i: rx_col[b, j, i], lambda w: rx_cor[b, j, w])

        for j in range(1 if early else DEPTH):
            arrive(j)

        @pl.when(following < BLOCKS)
        def _():
            for j in range(DEPTH):
                frame_copy(0, j).wait()

        todo = [t for j in range(DEPTH) for t in tasks(j)]
        build(xs.at[0], 0, todo[0])
        for i, task in enumerate(todo):
            if i + 1 < len(todo):
                if early and todo[i + 1][0] != task[0]:
                    arrive(todo[i + 1][0])
                build(xs.at[todo[i + 1][0]], (i + 1) % 2, todo[i + 1])
            j, _, n, width, at = task
            xg[j, at:at + n * width, :] = product(i % 2, task, wx) + bias[...]
            if i + 1 == len(todo) or todo[i + 1][0] != j:
                take_frame(following, j, range(PAIRS))
                pack_frame(following, j)

        @pl.when(following < BLOCKS)
        def _():
            for j in range(DEPTH):
                send(following, j, peers)

        @pl.when(following + 1 < BLOCKS)
        def _():
            for j in range(DEPTH):
                frame_copy((following + 1) * DEPTH + j, j).start()

    def cells(slot, task, t):
        j, first, n, width, base = task
        gts[slot, 0:n * width, :] = product(slot, task, wh) + xg[j, base:base + n * width, :]
        for q in range(n):
            rows_q = pl.ds(q * width, width)
            gi, gf, go, gg = (gts[slot, rows_q, 128 * i:128 * i + 128] for i in range(4))
            at = first + q
            c_old = cs[at - 1, 0:width, :]
            ti, tf, to = jnp.tanh(0.5 * gi), jnp.tanh(0.5 * gf), jnp.tanh(0.5 * go)
            c_new = 0.5 * ((tf + 1.0) * c_old + (ti + 1.0) * jnp.tanh(gg))
            cs[at - 1, 0:width, :] = c_new
            h_new = 0.5 * (to + 1.0) * jnp.tanh(c_new)
            if at < EDGE:
                h_new = h_new * up_mask
            if at >= EDGE + PAIRS:
                h_new = h_new * down_mask
            hs[at, 8:72, :] = h_new[0:OWN]
            hs[at, 80:88, :] = h_new[0:8]
            if width == 72:
                unpack_side(hs, at, h_new[64:72])
            if EDGE <= at < EDGE + PAIRS:
                for s in range(2):
                    both = hs[at, pl.ds(8 + s, 32, stride=2), :].astype(BF16)
                    h_out[t, s, 2 * (at - EDGE)] = both[:, 0:64]
                    h_out[t, s, 2 * (at - EDGE) + 1] = both[:, 64:128]

    def steps(b, sends):
        todo = [t for j in range(DEPTH) for t in tasks(j)]
        build(hs, 0, todo[0])
        for i, task in enumerate(todo):
            if i + 1 < len(todo):
                build(hs, (i + 1) % 2, todo[i + 1])
            cells(i % 2, task, b * DEPTH + task[0])
            if sends and i + 2 >= len(todo):
                send_state_cols(b + 1, i + 2 - len(todo))
        if sends:
            send_state_rest(b + 1)

    def weights(src, dst):
        zero = jnp.zeros((64, 64), BF16)
        for dx in range(3):
            for k, q in enumerate((0, 1, 2, -1)):
                for g in range(4):
                    parts = []
                    for p in range(2):
                        dy = q - p + 1
                        parts.append(src[dy, dx, :, 64 * g:64 * g + 64] if 0 <= dy <= 2 else zero)
                    dst[dx * 256 + k * 64:dx * 256 + k * 64 + 64, 128 * g:128 * g + 128] = jnp.concatenate(parts, axis=1)

    count = 3 + 2 * (has_up & has_down).astype(jnp.int32)
    for j in range(DEPTH):
        frame_copy(0, j).wait()
        take_frame(0, j, range(PAIRS))
        pack_frame(0, j)
        if j == 0:
            pl.semaphore_wait(barrier, count)
        send(0, j, peers)
    for j in range(DEPTH):
        frame_copy(DEPTH + j, j).start()
    for cp in inputs:
        cp.wait()
    ingest(lambda s, r: h_in[s, r], hs.at[pl.ds(EDGE, PAIRS), pl.ds(8, OWN)])
    ingest(lambda s, r: c_in[s, r], cs.at[pl.ds(1, PAIRS), pl.ds(0, OWN)])
    for q in range(PAIRS):
        wrap_first(hs, EDGE + q)
    for part in range(2):
        send_state_cols(0, part)
    send_state_rest(0)
    weights(wx_in, wx)
    weights(wh_in, wh)
    for g in range(4):
        piece = bias_in[:, 64 * g:64 * g + 64]
        bias[:, 128 * g:128 * g + 128] = jnp.concatenate([piece, piece], axis=1)
    conv_x(0, 1, early=True)

    def block(b, _):
        receive_state(b)
        steps(b, True)
        conv_x(b + 1, b + 2)
        return 0

    lax.fori_loop(0, BLOCKS - 1, block, 0)
    receive_state(BLOCKS - 1)
    steps(BLOCKS - 1, False)

    for q in range(PAIRS):
        for s in range(2):
            both = cs[1 + q, pl.ds(s, 32, stride=2), :]
            c_out[s, 2 * q] = both[:, 0:64]
            c_out[s, 2 * q + 1] = both[:, 64:128]

    def drain(b, _):
        for kind in range(DEPTH + 2):
            for cond, cp in copies(b, kind, peers).values():
                guarded(cond, lambda cp=cp: cp.wait_send())
        return 0

    lax.fori_loop(0, BLOCKS, drain, 0)


def write_out(h, c, h_out, c_out, sem):
    copies = [pltpu.make_async_copy(h.at[t], h_out.at[t], sem.at[t]) for t in range(STEPS)]
    copies.append(pltpu.make_async_copy(c, c_out, sem.at[STEPS]))
    for cp in copies:
        cp.start()
    for cp in copies:
        cp.wait()


def solution(mesh):
    frame_spec = P(None, "batch", "rows", "cols", None)
    state_spec = P("batch", "rows", "cols", None)

    def local_run(frames, w_x, w_h, gate_bias, h_init, c_init):
        vmem = pl.BlockSpec(memory_space=pltpu.VMEM)
        hbm = pl.BlockSpec(memory_space=pltpu.HBM)
        most = max(region(j)[1] * region(j)[2] for j in range(DEPTH))
        strips = [
            [(BLOCKS, DEPTH, 2, HP, OWN, 128), (BLOCKS, DEPTH, 8, 16, 128), (BLOCKS, DEPTH, 2, 16, 128)],
            [(BLOCKS, 2, HP, OWN, 128), (BLOCKS, 8, 16, 128), (BLOCKS, 2, 16, 128)],
            [(BLOCKS, 2, OWN, 128), (BLOCKS, PAIRS // 2, 8, 128), (BLOCKS, 2, 8, 128)],
        ]
        recv_bufs = [pltpu.VMEM(s, BF16 if k < 2 else F32) for k in range(3) for s in strips[k]]
        strips[0] = [(s[0] + 1,) + s[1:] for s in strips[0]]
        send_bufs = [pltpu.VMEM(s, BF16 if k < 2 else F32) for k in range(3) for s in strips[k]]
        h_pairs, c_pairs = pl.pallas_call(
            kernel,
            out_shape=(pltpu.VMEM(frames.shape, BF16), pltpu.VMEM(c_init.shape, F32)),
            in_specs=[hbm] * 6,
            out_specs=(vmem, vmem),
            scratch_shapes=[
                pltpu.VMEM((DEPTH,) + h_init.shape, BF16),
                pltpu.VMEM(w_x.shape, BF16),
                pltpu.VMEM(w_h.shape, BF16),
                pltpu.VMEM((1, 256), F32),
                pltpu.VMEM(h_init.shape, BF16),
                pltpu.VMEM(c_init.shape, F32),
                pltpu.VMEM((DEPTH, ROWS_ALL, SUBL, 128), F32),
                pltpu.VMEM((ROWS_ALL, SUBL, 128), F32),
                pltpu.VMEM((PAIRS + 2, 72, 128), F32),
                pltpu.VMEM((DEPTH, most, 512), F32),
                pltpu.VMEM((2, 512, 768), BF16),
                pltpu.VMEM((2, 512, 512), F32),
                pltpu.VMEM((768, 512), BF16),
                pltpu.VMEM((768, 512), BF16),
                pltpu.VMEM((1, 512), F32),
                *send_bufs, *recv_bufs,
                pltpu.SemaphoreType.DMA((DEPTH,)),
                pltpu.SemaphoreType.DMA((5,)),
                pltpu.SemaphoreType.DMA((BLOCKS, DEPTH + 2, 6)),
                pltpu.SemaphoreType.DMA((BLOCKS, DEPTH + 2, 6)),
            ],
            compiler_params=pltpu.CompilerParams(collective_id=0, has_side_effects=True, vmem_limit_bytes=56 * 2**20),
        )(frames, w_x, w_h, gate_bias.reshape(1, 256), h_init, c_init)
        return pl.pallas_call(
            write_out,
            out_shape=(jax.ShapeDtypeStruct(frames.shape, BF16), jax.ShapeDtypeStruct(c_init.shape, F32)),
            in_specs=[vmem, vmem],
            out_specs=(hbm, hbm),
            scratch_shapes=[pltpu.SemaphoreType.DMA((STEPS + 1,))],
            compiler_params=pltpu.CompilerParams(vmem_limit_bytes=16 * 2**20),
        )(h_pairs, c_pairs)

    return jax.shard_map(local_run, mesh=mesh, in_specs=(frame_spec, P(), P(), P(), state_spec, state_spec),
                         out_specs=(frame_spec, state_spec), check_vma=False)
```

time: 56.7 us -> 46.3 us (0.82)
  Pallas kernels: 55.7 us -> 45.4 us
    pallas_call x2, Pallas kernels: 55.7 us -> 45.4 us  [the longest x1 42.3 us: local_run(): pl.pallas_call(kernel, out_shape=(pltpu.VMEM(frames.shape, BF16), pltpu.V...]
where the time goes in v3:
time: 46.3 us; the launch traced here: 46.2 us
  Pallas kernels  45.4 us (98%)
  between operations  0.8 us (2%)
    pallas_call x1, Pallas kernels, local_run(): pl.pallas_call(kernel, out_shape=(pltpu.VMEM(frames.shape, BF16), pltpu.V...  42.3 us
    pallas_call x1, Pallas kernels, local_run(): pl.pallas_call(write_out, out_shape=(jax.ShapeDtypeStruct(frames.shape, B...  3.1 us

profile of v3, /device:TPU:0, one launch (start us, length us, event | category | flops | bytes accessed | tf_op | source)
XLA Modules:
  0.0 46.2 jit_solution(8538963492683101799)
XLA Ops:
  0.6 42.3 %shard_map.77 = (bf16[12,2,32,32,64]{4,3,2,1,0:T(8,128)(2,1)S(1)}, f32[2,32,32,64]{3,2,1,0:T(8,128)S(1)}) custom-call(bf16[12,2,32,32,64]{4,3,2,1,0:T(8,128)(2,1)} %frames.1, bf16[3,3,64,256]{3,2,1,0:T(8,128)(2,1)} %wx_hbm.1, bf16[3,3,64,256]{3,2,1,0:T(8,128)(2,1)} %wh_hbm.1, f32[1,256]{1,0:T(1,128)} %bitcast.1, bf16[2,32,32,64]{3,2,1,0:T(8,128)(2,1)} %h_hbm.1, ...), custom_call_target="tpu_custom_call" | custom-call | tf_op jit(solution)/shard_map/pallas_call | solution.py:407
  43.0 3.1 %shard_map.78 = (bf16[12,2,32,32,64]{4,3,2,1,0:T(8,128)(2,1)}, f32[2,32,32,64]{3,2,1,0:T(8,128)}) custom-call(bf16[12,2,32,32,64]{4,3,2,1,0:T(8,128)(2,1)S(1)} %get-tuple-element.4.h, f32[2,32,32,64]{3,2,1,0:T(8,128)S(1)} %get-tuple-element.5.c), custom_call_target="tpu_custom_call" | custom-call | tf_op jit(solution)/shard_map/pallas_call | solution.py:436

commit v4 on v3

--- a/solution.py
+++ b/solution.py
@@ -19,8 +19,9 @@
 HP = -(-DEPTH // 2)
 ROWS_ALL = PAIRS + 2 * EDGE
 SUBL = 88
-FROM_UP, FROM_DOWN, FROM_SIDE_A, FROM_SIDE_B, FROM_DUP, FROM_DDOWN = range(6)
-MIRROR = (FROM_DOWN, FROM_UP, FROM_SIDE_A, FROM_SIDE_B, FROM_DDOWN, FROM_DUP)
+FROM_UP, FROM_DOWN, FROM_SIDE, FROM_DUP, FROM_DDOWN = DIRS = range(5)
+MIRROR = (FROM_DOWN, FROM_UP, FROM_SIDE, FROM_DDOWN, FROM_DUP)
+FRAME, HID, CELL = range(3)
 
 
 def region(j):
@@ -30,28 +31,16 @@
 
 
 def kernel(frames, wx_hbm, wh_hbm, bias_hbm, h_hbm, c_hbm, h_out, c_out,
-           fbuf, wx_in, wh_in, bias_in, h_in, c_in, xs, hs, cs, xg, lhs, gts, wx, wh, bias,
+           fbuf, wx_in, wh_in, bias_in, h_in, c_in, xs, hs, cs, xg, gts, wx, wh, bias,
            sx_row, sx_col, sx_cor, sh_row, sh_col, sh_cor, sc_row, sc_col, sc_cor,
            rx_row, rx_col, rx_cor, rh_row, rh_col, rh_cor, rc_row, rc_col, rc_cor,
            fsem, isem, ssem, rsem):
     row, col, grp = lax.axis_index("rows"), lax.axis_index("cols"), lax.axis_index("batch")
-    n_rows = 4
+    n_rows = lax.axis_size("rows")
     side = 1 - col
     has_up, has_down = row > 0, row < n_rows - 1
-    peers = {
-        FROM_UP: (has_up, row - 1, col),
-        FROM_DOWN: (has_down, row + 1, col),
-        FROM_SIDE_A: (None, row, side),
-        FROM_SIDE_B: (None, row, side),
-        FROM_DUP: (has_up, row - 1, side),
-        FROM_DDOWN: (has_down, row + 1, side),
-    }
-
-    def guarded(cond, fn):
-        if cond is None:
-            fn()
-        else:
-            pl.when(cond)(fn)
+    above, below = lax.rem(row + n_rows - 1, n_rows), lax.rem(row + 1, n_rows)
+    peers = ((above, col), (below, col), (row, side), (above, side), (below, side))
 
     lane = lax.broadcasted_iota(jnp.int32, (72, 128), 1)
     subl = lax.broadcasted_iota(jnp.int32, (8, 128), 0)
@@ -71,10 +60,8 @@
         cp.start()
 
     barrier = pltpu.get_barrier_semaphore()
-    for d, (cond, r, c) in peers.items():
-        if d == FROM_SIDE_B:
-            continue
-        guarded(cond, lambda r=r, c=c: pl.semaphore_signal(barrier, inc=1, device_id=(grp, c, r), device_id_type=MESH))
+    for r, c in peers:
+        pl.semaphore_signal(barrier, inc=1, device_id=(grp, c, r), device_id_type=MESH)
 
     def ingest(load, dst):
         def body(i, _):
@@ -130,61 +117,81 @@
             unpack_side(dst, EDGE + 2 * i, both[0:8])
             unpack_side(dst, EDGE + 2 * i + 1, both[8:16])
 
-        def rows(which, first):
+        for which, first, mask in ((0, EDGE - HP, up_mask), (1, EDGE + PAIRS, down_mask)):
+            both = get_cor(which).astype(F32) * mask
             for p in range(HP):
-                strip = get_row(which, p).astype(F32)
+                strip = get_row(which, p).astype(F32) * mask
                 dst[first + p, 8:72, :] = strip
                 dst[first + p, 80:88, :] = strip[0:8]
-            both = get_cor(which).astype(F32)
-            for p in range(HP):
                 at = 2 - HP + p if which == 0 else p
                 unpack_side(dst, first + p, both[8 * at:8 * at + 8])
 
-        pl.when(has_up)(lambda: rows(0, EDGE - HP))
-        pl.when(has_down)(lambda: rows(1, EDGE + PAIRS))
-
-    def copies(b, kind, dirs, arriving=False):
-        (s_row, s_col, s_cor), (r_row, r_col, r_cor) = bufs(b, kind)
-        out = {}
-        for d in dirs:
-            cond, r, c = peers[d]
-            m = d if arriving else MIRROR[d]
-            if d in (FROM_UP, FROM_DOWN):
-                src, dst = s_row.at[d], r_row.at[m]
-            elif d in (FROM_SIDE_A, FROM_SIDE_B):
-                half = pl.ds(4 * (d - FROM_SIDE_A), 4)
-                src, dst = s_col.at[half], r_col.at[half]
+    def ends(sends, recvs, d, m):
+        (s_row, s_col, s_cor), (r_row, r_col, r_cor) = sends, recvs
+        if d in (FROM_UP, FROM_DOWN):
+            return s_row.at[d], r_row.at[m]
+        if d == FROM_SIDE:
+            return s_col, r_col
+        return s_cor.at[d - FROM_DUP], r_cor.at[m - FROM_DUP]
+
+    def remote(kind, b, j, d, m, src, dst):
+        r, c = peers[d]
+        return pltpu.make_async_remote_copy(
+            src_ref=src, dst_ref=dst, send_sem=ssem.at[kind, d], recv_sem=rsem.at[b, kind + j, m],
+            device_id=(grp, c, r), device_id_type=MESH)
+
+    send_bufs = ((sx_row, sx_col, sx_cor), (sh_row, sh_col, sh_cor), (sc_row, sc_col, sc_cor))
+    recv_bufs = ((rx_row, rx_col, rx_cor), (rh_row, rh_col, rh_cor), (rc_row, rc_col, rc_cor))
+
+    def frame_sem(b, j):
+        return 3 + j if isinstance(b, int) and b == 0 else 0
+
+    def send_frame(b, j):
+        for d in DIRS:
+            sends, recvs = ([x.at[b, j] for x in bufs[FRAME]] for bufs in (send_bufs, recv_bufs))
+            src, dst = ends(sends, recvs, d, MIRROR[d])
+            remote(FRAME, b, frame_sem(b, j), d, MIRROR[d], src, dst).start()
+
+    def receive_frames(b, j=None):
+        for d in DIRS:
+            if j is None:
+                at = (b, slice(None), d) if d < FROM_SIDE else (b,) if d == FROM_SIDE else (b, slice(None), d - FROM_DUP)
             else:
-                src, dst = s_cor.at[d - FROM_DUP], r_cor.at[m - FROM_DUP]
-            out[d] = (cond, pltpu.make_async_remote_copy(
-                src_ref=src, dst_ref=dst, send_sem=ssem.at[b, kind, d], recv_sem=rsem.at[b, kind, m],
-                device_id=(grp, c, r), device_id_type=MESH))
-        return out
-
-    def bufs(b, kind):
-        if kind < DEPTH:
-            return ((sx_row.at[b, kind], sx_col.at[b, kind], sx_cor.at[b, kind]),
-                    (rx_row.at[b, kind], rx_col.at[b, kind], rx_cor.at[b, kind]))
-        if kind == DEPTH:
-            return ((sh_row.at[b], sh_col.at[b], sh_cor.at[b]), (rh_row.at[b], rh_col.at[b], rh_cor.at[b]))
-        return ((sc_row.at[b], sc_col.at[b], sc_cor.at[b]), (rc_row.at[b], rc_col.at[b], rc_cor.at[b]))
-
-    OTHERS = (FROM_UP, FROM_DOWN, FROM_DUP, FROM_DDOWN)
-
-    def send(b, kind, dirs):
-        for cond, cp in copies(b, kind, dirs).values():
-            guarded(cond, lambda cp=cp: cp.start())
-
-    def receive(b, kind):
-        for cond, cp in copies(b, kind, peers, arriving=True).values():
-            guarded(cond, lambda cp=cp: cp.wait_recv())
+                at = (b, j, d) if d < FROM_SIDE else (b, j) if d == FROM_SIDE else (b, j, d - FROM_DUP)
+            which = 0 if d < FROM_SIDE else 1 if d == FROM_SIDE else 2
+            remote(FRAME, b, frame_sem(b, j or 0), d, d, send_bufs[FRAME][which].at[at], recv_bufs[FRAME][which].at[at]).wait_recv()
+
+    def send_state(kind, b, d, half=None):
+        sends, recvs = ([x.at[b] for x in bufs[kind]] for bufs in (send_bufs, recv_bufs))
+        src, dst = ends(sends, recvs, d, MIRROR[d])
+        if half is not None:
+            src, dst = src.at[pl.ds(4 * half, 4)], dst.at[pl.ds(4 * half, 4)]
+        remote(kind, b, 0, d, MIRROR[d], src, dst).start()
+
+    def receive_strips(b):
+        for kind in (HID, CELL):
+            for d in DIRS:
+                sends, recvs = ([x.at[b] for x in bufs[kind]] for bufs in (send_bufs, recv_bufs))
+                src, dst = ends(sends, recvs, d, d)
+                remote(kind, b, 0, d, d, src, dst).wait_recv()
+
+    def drain():
+        for kind in (FRAME, HID, CELL):
+            for d in DIRS:
+                which = 0 if d < FROM_SIDE else 1 if d == FROM_SIDE else 2
+                buf = send_bufs[kind][which]
+                at = [pl.ds(0, BLOCKS)] + ([slice(None)] if kind == FRAME else [])
+                if d != FROM_SIDE:
+                    at.append(d if d < FROM_SIDE else d - FROM_DUP)
+                whole, there = buf.at[tuple(at)], recv_bufs[kind][which].at[tuple(at)]
+                remote(kind, 0, 0, d, d, whole, there).wait_send()
 
     def send_state_cols(b, part):
         pack_cols(hs, sh_col.at[b], sh_cor.at[b], part)
         for q in range(8 * part, 8 * part + 8):
             sc_col[b, q // 2, 4 * (q % 2):4 * (q % 2) + 4] = cs[1 + q, pl.ds(cstrip_from, 4), :]
-        for kind in (DEPTH, DEPTH + 1):
-            send(b, kind, (FROM_SIDE_A + part,))
+        for kind in (HID, CELL):
+            send_state(kind, b, FROM_SIDE, part)
 
     def send_state_rest(b):
         pack_rows(hs, sh_row.at[b])
@@ -192,23 +199,18 @@
         sc_row[b, 1] = cs[PAIRS, 0:OWN, :]
         sc_cor[b, 0] = cs[1, pl.ds(cstrip_at, 8), :]
         sc_cor[b, 1] = cs[PAIRS, pl.ds(cstrip_at, 8), :]
-        for kind in (DEPTH, DEPTH + 1):
-            send(b, kind, OTHERS)
+        for kind in (HID, CELL):
+            for d in (FROM_UP, FROM_DOWN, FROM_DUP, FROM_DDOWN):
+                send_state(kind, b, d)
 
     def receive_state(b):
-        receive(b, DEPTH)
+        receive_strips(b)
         unpack_bf16(hs, lambda w, p: rh_row[b, w, p], lambda i: rh_col[b, i], lambda w: rh_cor[b, w])
-        if DEPTH > 1:
-            receive(b, DEPTH + 1)
-            for q in range(PAIRS):
-                cs[1 + q, pl.ds(cstrip_to, 4), :] = rc_col[b, q // 2, 4 * (q % 2):4 * (q % 2) + 4]
-
-            def rows(which, at):
-                cs[at, 0:OWN, :] = rc_row[b, which]
-                cs[at, 64:72, :] = rc_cor[b, which]
-
-            pl.when(has_up)(lambda: rows(0, 0))
-            pl.when(has_down)(lambda: rows(1, 1 + PAIRS))
+        for q in range(PAIRS):
+            cs[1 + q, pl.ds(cstrip_to, 4), :] = rc_col[b, q // 2, 4 * (q % 2):4 * (q % 2) + 4]
+        for which, at in ((0, 0), (1, 1 + PAIRS)):
+            cs[at, 0:OWN, :] = rc_row[b, which]
+            cs[at, 64:72, :] = rc_cor[b, which]
 
     def take_frame(b, j, pairs):
         for q in pairs:
@@ -227,61 +229,55 @@
         n = 6 if count == 18 else 8
         return [(j, first + g, n, width, g * width) for g in range(0, count, n)]
 
-    def build(src, slot, task):
+    def product(src, task, w):
         _, first, n, width, _ = task
         low = (lane < 64)[0:width]
-        for q in range(0, n, 2):
-            for dx in range(3):
-                at = pl.ds(6 + 2 * dx, width)
-                r = [src[first + q + i, at, :] for i in range(-1, 3)]
-                own = jnp.concatenate([r[1], r[2]], axis=0).astype(BF16)
-                near = jnp.concatenate([jnp.where(low, r[2], r[0]), jnp.where(low, r[3], r[1])], axis=0).astype(BF16)
-                lhs[slot, q * width:(q + 2) * width, dx * 256:dx * 256 + 128] = own
-                lhs[slot, q * width:(q + 2) * width, dx * 256 + 128:dx * 256 + 256] = near
-
-    def product(slot, task, w):
-        _, _, n, width, _ = task
-        return jnp.dot(lhs[slot, 0:n * width, :], w[...], preferred_element_type=F32)
-
-    def conv_x(b, following, early=False):
-        def arrive(j):
-            receive(b, j)
-            unpack_bf16(xs.at[j], lambda w, p: rx_row[b, j, w, p], lambda i: rx_col[b, j, i], lambda w: rx_cor[b, j, w])
-
-        for j in range(1 if early else DEPTH):
-            arrive(j)
-
-        @pl.when(following < BLOCKS)
-        def _():
+        total = None
+        for dx in range(3):
+            at = pl.ds(6 + 2 * dx, width)
+            r = [src[first + i, at, :] for i in range(-1, n + 1)]
+            own = jnp.concatenate(r[1:n + 1], axis=0).astype(BF16)
+            near = jnp.concatenate([jnp.where(low, r[i + 2], r[i]) for i in range(n)], axis=0).astype(BF16)
+            part = jnp.dot(jnp.concatenate([own, near], axis=1), w[dx * 256:dx * 256 + 256, :], preferred_element_type=F32)
+            total = part if total is None else total + part
+        return total
+
+    def unpack_frame(b, j):
+        unpack_bf16(xs.at[j], lambda w, p: rx_row[b, j, w, p], lambda i: rx_col[b, j, i], lambda w: rx_cor[b, j, w])
+
+    def x_gates(src, slot, task):
+        j, _, n, width, at = task
+        xg[j, at:at + n * width, :] = product(src, task, wx) + bias[...]
+
+    all_tasks = [t for j in range(DEPTH) for t in tasks(j)]
+    last_of_step = [i + 1 == len(all_tasks) or all_tasks[i + 1][0] != t[0] for i, t in enumerate(all_tasks)]
+
+    def frames_wait(following):
+        for j in range(DEPTH):
+            frame_copy(0, j).wait()
+
+    def frames_on(following):
+        def sends():
             for j in range(DEPTH):
-                frame_copy(0, j).wait()
-
-        todo = [t for j in range(DEPTH) for t in tasks(j)]
-        build(xs.at[0], 0, todo[0])
-        for i, task in enumerate(todo):
-            if i + 1 < len(todo):
-                if early and todo[i + 1][0] != task[0]:
-                    arrive(todo[i + 1][0])
-                build(xs.at[todo[i + 1][0]], (i + 1) % 2, todo[i + 1])
-            j, _, n, width, at = task
-            xg[j, at:at + n * width, :] = product(i % 2, task, wx) + bias[...]
-            if i + 1 == len(todo) or todo[i + 1][0] != j:
-                take_frame(following, j, range(PAIRS))
-                pack_frame(following, j)
-
-        @pl.when(following < BLOCKS)
-        def _():
-            for j in range(DEPTH):
-                send(following, j, peers)
-
-        @pl.when(following + 1 < BLOCKS)
-        def _():
+                send_frame(following, j)
+
+        def fetches():
             for j in range(DEPTH):
                 frame_copy((following + 1) * DEPTH + j, j).start()
 
+        if isinstance(following, int):
+            sends()
+            fetches()
+        else:
+            pl.when(following < BLOCKS)(sends)
+            pl.when(following + 1 < BLOCKS)(fetches)
+
+    def h_gates(src, slot, task):
+        j, _, n, width, base = task
+        gts[slot, 0:n * width, :] = product(src, task, wh) + xg[j, base:base + n * width, :]
+
     def cells(slot, task, t):
         j, first, n, width, base = task
-        gts[slot, 0:n * width, :] = product(slot, task, wh) + xg[j, base:base + n * width, :]
         for q in range(n):
             rows_q = pl.ds(q * width, width)
             gi, gf, go, gg = (gts[slot, rows_q, 128 * i:128 * i + 128] for i in range(4))
@@ -305,17 +301,36 @@
                     h_out[t, s, 2 * (at - EDGE)] = both[:, 0:64]
                     h_out[t, s, 2 * (at - EDGE) + 1] = both[:, 64:128]
 
-    def steps(b, sends):
-        todo = [t for j in range(DEPTH) for t in tasks(j)]
-        build(hs, 0, todo[0])
-        for i, task in enumerate(todo):
+    def run(hid_block, x_block):
+        todo = []
+        if hid_block is not None:
+            todo += [(hs, t, True) for t in all_tasks]
+        if x_block is not None:
+            todo += [(xs.at[t[0]], t, False) for t in all_tasks]
+        def ahead(i):
+            src, task, hidden = todo[i]
+            (h_gates if hidden else x_gates)(src, i % 2, task)
+
+        ahead(0)
+        for i, (src, task, hidden) in enumerate(todo):
+            n = i % len(all_tasks)
+            if hidden and x_block is not None and n + 1 == len(all_tasks):
+                for j in range(DEPTH):
+                    unpack_frame(x_block, j)
             if i + 1 < len(todo):
-                build(hs, (i + 1) % 2, todo[i + 1])
-            cells(i % 2, task, b * DEPTH + task[0])
-            if sends and i + 2 >= len(todo):
-                send_state_cols(b + 1, i + 2 - len(todo))
-        if sends:
-            send_state_rest(b + 1)
+                ahead(i + 1)
+            if hidden:
+                cells(i % 2, task, hid_block * DEPTH + task[0])
+                if x_block is not None:
+                    if n + 2 >= len(all_tasks):
+                        send_state_cols(hid_block + 1, n + 2 - len(all_tasks))
+                    if n + 2 == len(all_tasks):
+                        receive_frames(x_block)
+                    if n + 1 == len(all_tasks):
+                        send_state_rest(hid_block + 1)
+            elif last_of_step[n]:
+                take_frame(x_block + 1, task[0], range(PAIRS))
+                pack_frame(x_block + 1, task[0])
 
     def weights(src, dst):
         zero = jnp.zeros((64, 64), BF16)
@@ -328,14 +343,13 @@
                         parts.append(src[dy, dx, :, 64 * g:64 * g + 64] if 0 <= dy <= 2 else zero)
                     dst[dx * 256 + k * 64:dx * 256 + k * 64 + 64, 128 * g:128 * g + 128] = jnp.concatenate(parts, axis=1)
 
-    count = 3 + 2 * (has_up & has_down).astype(jnp.int32)
     for j in range(DEPTH):
         frame_copy(0, j).wait()
         take_frame(0, j, range(PAIRS))
         pack_frame(0, j)
         if j == 0:
-            pl.semaphore_wait(barrier, count)
-        send(0, j, peers)
+            pl.semaphore_wait(barrier, len(peers))
+        send_frame(0, j)
     for j in range(DEPTH):
         frame_copy(DEPTH + j, j).start()
     for cp in inputs:
@@ -352,17 +366,28 @@
     for g in range(4):
         piece = bias_in[:, 64 * g:64 * g + 64]
         bias[:, 128 * g:128 * g + 128] = jnp.concatenate([piece, piece], axis=1)
-    conv_x(0, 1, early=True)
+    for j in range(DEPTH):
+        receive_frames(0, j)
+        unpack_frame(0, j)
+        if j == DEPTH - 1:
+            frames_wait(1)
+        for task in tasks(j):
+            x_gates(xs.at[j], 0, task)
+    for j in range(DEPTH):
+        take_frame(1, j, range(PAIRS))
+        pack_frame(1, j)
+    frames_on(1)
 
     def block(b, _):
+        pl.when(b + 2 < BLOCKS)(lambda: frames_wait(b + 2))
         receive_state(b)
-        steps(b, True)
-        conv_x(b + 1, b + 2)
+        run(b, b + 1)
+        frames_on(b + 2)
         return 0
 
     lax.fori_loop(0, BLOCKS - 1, block, 0)
     receive_state(BLOCKS - 1)
-    steps(BLOCKS - 1, False)
+    run(BLOCKS - 1, None)
 
     for q in range(PAIRS):
         for s in range(2):
@@ -370,13 +395,7 @@
             c_out[s, 2 * q] = both[:, 0:64]
             c_out[s, 2 * q + 1] = both[:, 64:128]
 
-    def drain(b, _):
-        for kind in range(DEPTH + 2):
-            for cond, cp in copies(b, kind, peers).values():
-                guarded(cond, lambda cp=cp: cp.wait_send())
-        return 0
-
-    lax.fori_loop(0, BLOCKS, drain, 0)
+    drain()
 
 
 def write_out(h, c, h_out, c_out, sem):
@@ -420,7 +439,6 @@
                 pltpu.VMEM((ROWS_ALL, SUBL, 128), F32),
                 pltpu.VMEM((PAIRS + 2, 72, 128), F32),
                 pltpu.VMEM((DEPTH, most, 512), F32),
-                pltpu.VMEM((2, 512, 768), BF16),
                 pltpu.VMEM((2, 512, 512), F32),
                 pltpu.VMEM((768, 512), BF16),
                 pltpu.VMEM((768, 512), BF16),
@@ -428,8 +446,8 @@
                 *send_bufs, *recv_bufs,
                 pltpu.SemaphoreType.DMA((DEPTH,)),
                 pltpu.SemaphoreType.DMA((5,)),
-                pltpu.SemaphoreType.DMA((BLOCKS, DEPTH + 2, 6)),
-                pltpu.SemaphoreType.DMA((BLOCKS, DEPTH + 2, 6)),
+                pltpu.SemaphoreType.DMA((3, 5)),
+                pltpu.SemaphoreType.DMA((BLOCKS, 3 + DEPTH, 5)),
             ],
             compiler_params=pltpu.CompilerParams(collective_id=0, has_side_effects=True, vmem_limit_bytes=56 * 2**20),
         )(frames, w_x, w_h, gate_bias.reshape(1, 256), h_init, c_init)

time: 46.3 us -> 45.2 us (0.976)
  Pallas kernels: 45.4 us -> 44.4 us
    pallas_call x1, Pallas kernels: 42.3 us -> 41.3 us  [local_run(): pl.pallas_call(kernel, out_shape=(pltpu.VMEM(frames.shape, BF16), pltpu.V...]
where the time goes in v4:
time: 45.2 us; the launch traced here: 45 us
  Pallas kernels  44.4 us (98%)
  between operations  0.64 us (1%)
    pallas_call x1, Pallas kernels, local_run(): pl.pallas_call(kernel, out_shape=(pltpu.VMEM(frames.shape, BF16), pltpu.V...  41.3 us
    pallas_call x1, Pallas kernels, local_run(): pl.pallas_call(write_out, out_shape=(jax.ShapeDtypeStruct(frames.shape, B...  3.1 us

profile of v4, /device:TPU:0, one launch (start us, length us, event | category | flops | bytes accessed | tf_op | source)
XLA Modules:
  0.0 45.0 jit_solution(9513781930627275779)
XLA Ops:
  0.6 41.3 %shard_map.77 = (bf16[12,2,32,32,64]{4,3,2,1,0:T(8,128)(2,1)S(1)}, f32[2,32,32,64]{3,2,1,0:T(8,128)S(1)}) custom-call(bf16[12,2,32,32,64]{4,3,2,1,0:T(8,128)(2,1)} %frames.1, bf16[3,3,64,256]{3,2,1,0:T(8,128)(2,1)} %wx_hbm.1, bf16[3,3,64,256]{3,2,1,0:T(8,128)(2,1)} %wh_hbm.1, f32[1,256]{1,0:T(1,128)} %bitcast.1, bf16[2,32,32,64]{3,2,1,0:T(8,128)(2,1)} %h_hbm.1, ...), custom_call_target="tpu_custom_call" | custom-call | tf_op jit(solution)/shard_map/pallas_call | solution.py:426
  41.9 3.1 %shard_map.78 = (bf16[12,2,32,32,64]{4,3,2,1,0:T(8,128)(2,1)}, f32[2,32,32,64]{3,2,1,0:T(8,128)}) custom-call(bf16[12,2,32,32,64]{4,3,2,1,0:T(8,128)(2,1)S(1)} %get-tuple-element.4.h, f32[2,32,32,64]{3,2,1,0:T(8,128)S(1)} %get-tuple-element.5.c), custom_call_target="tpu_custom_call" | custom-call | tf_op jit(solution)/shard_map/pallas_call | solution.py:454

commit v5 on v4

--- a/solution.py
+++ b/solution.py
@@ -22,6 +22,7 @@
 FROM_UP, FROM_DOWN, FROM_SIDE, FROM_DUP, FROM_DDOWN = DIRS = range(5)
 MIRROR = (FROM_DOWN, FROM_UP, FROM_SIDE, FROM_DDOWN, FROM_DUP)
 FRAME, HID, CELL = range(3)
+COL_ORDER = (0, 1, 6, 7, 2, 3, 4, 5)
 
 
 def region(j):
@@ -60,8 +61,16 @@
         cp.start()
 
     barrier = pltpu.get_barrier_semaphore()
-    for r, c in peers:
-        pl.semaphore_signal(barrier, inc=1, device_id=(grp, c, r), device_id_type=MESH)
+    def toward(fn):
+        def both(a, b):
+            fn(a)
+            fn(b)
+
+        fn(FROM_SIDE)
+        pl.when(has_up)(lambda: both(FROM_UP, FROM_DUP))
+        pl.when(has_down)(lambda: both(FROM_DOWN, FROM_DDOWN))
+
+    toward(lambda d: pl.semaphore_signal(barrier, inc=1, device_id=(grp, peers[d][1], peers[d][0]), device_id_type=MESH))
 
     def ingest(load, dst):
         def body(i, _):
@@ -85,6 +94,9 @@
         cs[q] = nil[0:72]
     for q in range(PAIRS):
         cs[1 + q, 64:72, :] = nil[0:8]
+        for j in range(1, DEPTH):
+            xs[j, EDGE + q, 0:8, :] = nil[0:8]
+            xs[j, EDGE + q, 72:80, :] = nil[0:8]
 
     strip_at = pl.multiple_of(8 + 56 * (1 - col), 8)
     cstrip_at = pl.multiple_of(56 * (1 - col), 8)
@@ -97,30 +109,53 @@
             s_row[1, p] = src[EDGE + PAIRS - HP + p, 8:72, :].astype(BF16)
 
     def pack_cols(src, s_col, s_cor, part):
-        for i in range(4 * part, 4 * part + 4):
+        for at, i in list(enumerate(COL_ORDER))[4 * part:4 * part + 4]:
             two = jnp.concatenate([src[EDGE + 2 * i, pl.ds(strip_at, 8), :],
                                    src[EDGE + 2 * i + 1, pl.ds(strip_at, 8), :]], axis=0).astype(BF16)
-            s_col[i] = two
+            s_col[at] = two
             if i == 0:
                 s_cor[0] = two
             if i == PAIRS // 2 - 1:
                 s_cor[1] = two
 
+    def pack_narrow(src, s_row, s_col, s_cor):
+        s_row[0, 0] = src[EDGE, 8:72, :].astype(BF16)
+        s_row[1, 0] = src[EDGE + PAIRS - 1, 8:72, :].astype(BF16)
+        for i in range(PAIRS // 4):
+            s_col[i] = jnp.concatenate([src[EDGE + 4 * i + u, pl.ds(8 + cstrip_from, 4), :] for u in range(4)],
+                                       axis=0).astype(BF16)
+        for side_of, at in ((0, EDGE), (1, EDGE + PAIRS - 1)):
+            edge = src[at, pl.ds(strip_at, 8), :]
+            s_cor[side_of] = jnp.concatenate([edge, edge], axis=0).astype(BF16)
+
+    def unpack_narrow(dst, get_row, get_col, get_cor):
+        for i in range(PAIRS // 4):
+            four = get_col(i).astype(F32)
+            for u in range(4):
+                strip = four[4 * u:4 * u + 4]
+                dst[EDGE + 4 * i + u, pl.ds(8 + cstrip_to, 4), :] = strip
+                dst[EDGE + 4 * i + u, pl.ds(cstrip_to - 64, 4), :] = strip
+        for which, at, there in ((0, EDGE - 1, has_up), (1, EDGE + PAIRS, has_down)):
+            strip = jnp.where(there, get_row(which).astype(F32), 0.0)
+            dst[at, 8:72, :] = strip
+            dst[at, 80:88, :] = strip[0:8]
+            unpack_side(dst, at, jnp.where(there, get_cor(which).astype(F32)[0:8], 0.0))
+
     def unpack_side(dst, q, strip):
         strip = strip * col_mask
         dst[q, 72:80, :] = strip
         dst[q, 0:8, :] = strip
 
     def unpack_bf16(dst, get_row, get_col, get_cor):
-        for i in range(PAIRS // 2):
-            both = get_col(i).astype(F32)
+        for at, i in enumerate(COL_ORDER):
+            both = get_col(at).astype(F32)
             unpack_side(dst, EDGE + 2 * i, both[0:8])
             unpack_side(dst, EDGE + 2 * i + 1, both[8:16])
 
-        for which, first, mask in ((0, EDGE - HP, up_mask), (1, EDGE + PAIRS, down_mask)):
-            both = get_cor(which).astype(F32) * mask
+        for which, first, there in ((0, EDGE - HP, has_up), (1, EDGE + PAIRS, has_down)):
+            both = jnp.where(there, get_cor(which).astype(F32), 0.0)
             for p in range(HP):
-                strip = get_row(which, p).astype(F32) * mask
+                strip = jnp.where(there, get_row(which, p).astype(F32), 0.0)
                 dst[first + p, 8:72, :] = strip
                 dst[first + p, 80:88, :] = strip[0:8]
                 at = 2 - HP + p if which == 0 else p
@@ -137,29 +172,26 @@
     def remote(kind, b, j, d, m, src, dst):
         r, c = peers[d]
         return pltpu.make_async_remote_copy(
-            src_ref=src, dst_ref=dst, send_sem=ssem.at[kind, d], recv_sem=rsem.at[b, kind + j, m],
+            src_ref=src, dst_ref=dst, send_sem=ssem.at[kind + j, d], recv_sem=rsem.at[b, kind + j, m],
             device_id=(grp, c, r), device_id_type=MESH)
 
     send_bufs = ((sx_row, sx_col, sx_cor), (sh_row, sh_col, sh_cor), (sc_row, sc_col, sc_cor))
     recv_bufs = ((rx_row, rx_col, rx_cor), (rh_row, rh_col, rh_cor), (rc_row, rc_col, rc_cor))
 
-    def frame_sem(b, j):
-        return 3 + j if isinstance(b, int) and b == 0 else 0
-
-    def send_frame(b, j):
-        for d in DIRS:
-            sends, recvs = ([x.at[b, j] for x in bufs[FRAME]] for bufs in (send_bufs, recv_bufs))
-            src, dst = ends(sends, recvs, d, MIRROR[d])
-            remote(FRAME, b, frame_sem(b, j), d, MIRROR[d], src, dst).start()
-
-    def receive_frames(b, j=None):
-        for d in DIRS:
-            if j is None:
-                at = (b, slice(None), d) if d < FROM_SIDE else (b,) if d == FROM_SIDE else (b, slice(None), d - FROM_DUP)
-            else:
-                at = (b, j, d) if d < FROM_SIDE else (b, j) if d == FROM_SIDE else (b, j, d - FROM_DUP)
-            which = 0 if d < FROM_SIDE else 1 if d == FROM_SIDE else 2
-            remote(FRAME, b, frame_sem(b, j or 0), d, d, send_bufs[FRAME][which].at[at], recv_bufs[FRAME][which].at[at]).wait_recv()
+    def frame_ends(b, j, d, m):
+        sends, recvs = ([x.at[b, j] for x in bufs[FRAME]] for bufs in (send_bufs, recv_bufs))
+        src, dst = ends(sends, recvs, d, m)
+        if j and d < FROM_SIDE:
+            src, dst = src.at[pl.ds(0, 1)], dst.at[pl.ds(0, 1)]
+        if j and d == FROM_SIDE:
+            src, dst = src.at[pl.ds(0, 4)], dst.at[pl.ds(0, 4)]
+        return src, dst
+
+    def frame_out(b, j, d):
+        remote(FRAME, b, 3 + j, d, MIRROR[d], *frame_ends(b, j, d, MIRROR[d])).start()
+
+    def frame_in(b, j, d):
+        remote(FRAME, b, 3 + j, d, d, *frame_ends(b, j, d, d)).wait_recv()
 
     def send_state(kind, b, d, half=None):
         sends, recvs = ([x.at[b] for x in bufs[kind]] for bufs in (send_bufs, recv_bufs))
@@ -168,28 +200,32 @@
             src, dst = src.at[pl.ds(4 * half, 4)], dst.at[pl.ds(4 * half, 4)]
         remote(kind, b, 0, d, MIRROR[d], src, dst).start()
 
-    def receive_strips(b):
+    def state_in(b, d):
         for kind in (HID, CELL):
-            for d in DIRS:
-                sends, recvs = ([x.at[b] for x in bufs[kind]] for bufs in (send_bufs, recv_bufs))
-                src, dst = ends(sends, recvs, d, d)
-                remote(kind, b, 0, d, d, src, dst).wait_recv()
-
-    def drain():
-        for kind in (FRAME, HID, CELL):
-            for d in DIRS:
-                which = 0 if d < FROM_SIDE else 1 if d == FROM_SIDE else 2
-                buf = send_bufs[kind][which]
-                at = [pl.ds(0, BLOCKS)] + ([slice(None)] if kind == FRAME else [])
-                if d != FROM_SIDE:
-                    at.append(d if d < FROM_SIDE else d - FROM_DUP)
-                whole, there = buf.at[tuple(at)], recv_bufs[kind][which].at[tuple(at)]
-                remote(kind, 0, 0, d, d, whole, there).wait_send()
+            sends, recvs = ([x.at[b] for x in bufs[kind]] for bufs in (send_bufs, recv_bufs))
+            src, dst = ends(sends, recvs, d, d)
+            remote(kind, b, 0, d, d, src, dst).wait_recv()
+
+    def drain(d):
+        which = 0 if d < FROM_SIDE else 1 if d == FROM_SIDE else 2
+        for kind in (HID, CELL):
+            at = (slice(None),) + (() if d == FROM_SIDE else (d if d < FROM_SIDE else d - FROM_DUP,))
+            remote(kind, 0, 0, d, d, send_bufs[kind][which].at[at], recv_bufs[kind][which].at[at]).wait_send()
+        for j in range(DEPTH):
+            frame_in(BLOCKS, j, d)
+            if d == FROM_SIDE:
+                at = (slice(None), j) + ((pl.ds(0, 4),) if j else ())
+            elif d < FROM_SIDE:
+                at = (slice(None), j, d) + ((pl.ds(0, 1),) if j else ())
+            else:
+                at = (slice(None), j, d - FROM_DUP)
+            remote(FRAME, 0, 3 + j, d, d, send_bufs[FRAME][which].at[at], recv_bufs[FRAME][which].at[at]).wait_send()
 
     def send_state_cols(b, part):
         pack_cols(hs, sh_col.at[b], sh_cor.at[b], part)
-        for q in range(8 * part, 8 * part + 8):
-            sc_col[b, q // 2, 4 * (q % 2):4 * (q % 2) + 4] = cs[1 + q, pl.ds(cstrip_from, 4), :]
+        for at, i in list(enumerate(COL_ORDER))[4 * part:4 * part + 4]:
+            for u in range(2):
+                sc_col[b, at, 4 * u:4 * u + 4] = cs[1 + 2 * i + u, pl.ds(cstrip_from, 4), :]
         for kind in (HID, CELL):
             send_state(kind, b, FROM_SIDE, part)
 
@@ -199,18 +235,23 @@
         sc_row[b, 1] = cs[PAIRS, 0:OWN, :]
         sc_cor[b, 0] = cs[1, pl.ds(cstrip_at, 8), :]
         sc_cor[b, 1] = cs[PAIRS, pl.ds(cstrip_at, 8), :]
-        for kind in (HID, CELL):
-            for d in (FROM_UP, FROM_DOWN, FROM_DUP, FROM_DDOWN):
-                send_state(kind, b, d)
+
+        def out(d):
+            if d != FROM_SIDE:
+                for kind in (HID, CELL):
+                    send_state(kind, b, d)
+
+        toward(out)
 
     def receive_state(b):
-        receive_strips(b)
+        toward(lambda d: state_in(b, d))
         unpack_bf16(hs, lambda w, p: rh_row[b, w, p], lambda i: rh_col[b, i], lambda w: rh_cor[b, w])
-        for q in range(PAIRS):
-            cs[1 + q, pl.ds(cstrip_to, 4), :] = rc_col[b, q // 2, 4 * (q % 2):4 * (q % 2) + 4]
-        for which, at in ((0, 0), (1, 1 + PAIRS)):
-            cs[at, 0:OWN, :] = rc_row[b, which]
-            cs[at, 64:72, :] = rc_cor[b, which]
+        for at, i in enumerate(COL_ORDER):
+            for u in range(2):
+                cs[1 + 2 * i + u, pl.ds(cstrip_to, 4), :] = rc_col[b, at, 4 * u:4 * u + 4]
+        for which, at, there in ((0, 0, has_up), (1, 1 + PAIRS, has_down)):
+            cs[at, 0:OWN, :] = jnp.where(there, rc_row[b, which], 0.0)
+            cs[at, 64:72, :] = jnp.where(there, rc_cor[b, which], 0.0)
 
     def take_frame(b, j, pairs):
         for q in pairs:
@@ -220,34 +261,47 @@
             wrap_first(xs.at[j], EDGE + q)
 
     def pack_frame(b, j):
+        if j:
+            pack_narrow(xs.at[j], sx_row.at[b, j], sx_col.at[b, j], sx_cor.at[b, j])
+            return
         pack_rows(xs.at[j], sx_row.at[b, j])
         for part in range(2):
             pack_cols(xs.at[j], sx_col.at[b, j], sx_cor.at[b, j], part)
 
     def tasks(j):
         first, count, width = region(j)
-        n = 6 if count == 18 else 8
-        return [(j, first + g, n, width, g * width) for g in range(0, count, n)]
+        if count == 18:
+            lists = ((1, 2, 3, 16, 17, 18), (4, 5, 6, 13, 14, 15), (7, 8, 9, 10, 11, 12))
+        else:
+            lists = ((2, 3, 4, 5, 14, 15, 16, 17), (6, 7, 8, 9, 10, 11, 12, 13))
+        out, base = [], 0
+        for pairs in lists:
+            out.append((j, pairs, width, base))
+            base += len(pairs) * width
+        return out
 
     def product(src, task, w):
-        _, first, n, width, _ = task
+        _, pairs, width, _ = task
         low = (lane < 64)[0:width]
         total = None
         for dx in range(3):
             at = pl.ds(6 + 2 * dx, width)
-            r = [src[first + i, at, :] for i in range(-1, n + 1)]
-            own = jnp.concatenate(r[1:n + 1], axis=0).astype(BF16)
-            near = jnp.concatenate([jnp.where(low, r[i + 2], r[i]) for i in range(n)], axis=0).astype(BF16)
+            r = {q: src[q, at, :] for q in sorted({p + e for p in pairs for e in (-1, 0, 1)})}
+            own = jnp.concatenate([r[q] for q in pairs], axis=0).astype(BF16)
+            near = jnp.concatenate([jnp.where(low, r[q + 1], r[q - 1]) for q in pairs], axis=0).astype(BF16)
             part = jnp.dot(jnp.concatenate([own, near], axis=1), w[dx * 256:dx * 256 + 256, :], preferred_element_type=F32)
             total = part if total is None else total + part
         return total
 
     def unpack_frame(b, j):
+        if j:
+            unpack_narrow(xs.at[j], lambda w: rx_row[b, j, w, 0], lambda i: rx_col[b, j, i], lambda w: rx_cor[b, j, w])
+            return
         unpack_bf16(xs.at[j], lambda w, p: rx_row[b, j, w, p], lambda i: rx_col[b, j, i], lambda w: rx_cor[b, j, w])
 
     def x_gates(src, slot, task):
-        j, _, n, width, at = task
-        xg[j, at:at + n * width, :] = product(src, task, wx) + bias[...]
+        j, pairs, width, at = task
+        xg[j, at:at + len(pairs) * width, :] = product(src, task, wx) + bias[...]
 
     all_tasks = [t for j in range(DEPTH) for t in tasks(j)]
     last_of_step = [i + 1 == len(all_tasks) or all_tasks[i + 1][0] != t[0] for i, t in enumerate(all_tasks)]
@@ -256,32 +310,20 @@
         for j in range(DEPTH):
             frame_copy(0, j).wait()
 
-    def frames_on(following):
-        def sends():
-            for j in range(DEPTH):
-                send_frame(following, j)
-
-        def fetches():
-            for j in range(DEPTH):
-                frame_copy((following + 1) * DEPTH + j, j).start()
-
-        if isinstance(following, int):
-            sends()
-            fetches()
-        else:
-            pl.when(following < BLOCKS)(sends)
-            pl.when(following + 1 < BLOCKS)(fetches)
+    def fetch(b):
+        for j in range(DEPTH):
+            frame_copy(b * DEPTH + j, j).start()
 
     def h_gates(src, slot, task):
-        j, _, n, width, base = task
-        gts[slot, 0:n * width, :] = product(src, task, wh) + xg[j, base:base + n * width, :]
+        j, pairs, width, base = task
+        rows = len(pairs) * width
+        gts[slot, 0:rows, :] = product(src, task, wh) + xg[j, base:base + rows, :]
 
     def cells(slot, task, t):
-        j, first, n, width, base = task
-        for q in range(n):
+        j, pairs, width, _ = task
+        for q, at in enumerate(pairs):
             rows_q = pl.ds(q * width, width)
             gi, gf, go, gg = (gts[slot, rows_q, 128 * i:128 * i + 128] for i in range(4))
-            at = first + q
             c_old = cs[at - 1, 0:width, :]
             ti, tf, to = jnp.tanh(0.5 * gi), jnp.tanh(0.5 * gf), jnp.tanh(0.5 * go)
             c_new = 0.5 * ((tf + 1.0) * c_old + (ti + 1.0) * jnp.tanh(gg))
@@ -321,16 +363,19 @@
                 ahead(i + 1)
             if hidden:
                 cells(i % 2, task, hid_block * DEPTH + task[0])
-                if x_block is not None:
-                    if n + 2 >= len(all_tasks):
-                        send_state_cols(hid_block + 1, n + 2 - len(all_tasks))
-                    if n + 2 == len(all_tasks):
-                        receive_frames(x_block)
-                    if n + 1 == len(all_tasks):
-                        send_state_rest(hid_block + 1)
+                if x_block is not None and n + 2 == len(all_tasks):
+                    send_state_cols(hid_block + 1, 0)
+                    send_state_rest(hid_block + 1)
+                    toward(lambda d: [frame_in(x_block, j, d) for j in range(DEPTH)])
+                if x_block is not None and n + 1 == len(all_tasks):
+                    send_state_cols(hid_block + 1, 1)
             elif last_of_step[n]:
                 take_frame(x_block + 1, task[0], range(PAIRS))
                 pack_frame(x_block + 1, task[0])
+                if task[0] == 1:
+                    toward(lambda d: [frame_out(x_block + 1, j, d) for j in (0, 1)])
+                if task[0] == 2:
+                    toward(lambda d: frame_out(x_block + 1, 2, d))
 
     def weights(src, dst):
         zero = jnp.zeros((64, 64), BF16)
@@ -348,8 +393,8 @@
         take_frame(0, j, range(PAIRS))
         pack_frame(0, j)
         if j == 0:
-            pl.semaphore_wait(barrier, len(peers))
-        send_frame(0, j)
+            pl.semaphore_wait(barrier, 3 + 2 * (has_up & has_down).astype(jnp.int32))
+        toward(lambda d: frame_out(0, j, d))
     for j in range(DEPTH):
         frame_copy(DEPTH + j, j).start()
     for cp in inputs:
@@ -367,7 +412,7 @@
         piece = bias_in[:, 64 * g:64 * g + 64]
         bias[:, 128 * g:128 * g + 128] = jnp.concatenate([piece, piece], axis=1)
     for j in range(DEPTH):
-        receive_frames(0, j)
+        toward(lambda d: frame_in(0, j, d))
         unpack_frame(0, j)
         if j == DEPTH - 1:
             frames_wait(1)
@@ -376,13 +421,14 @@
     for j in range(DEPTH):
         take_frame(1, j, range(PAIRS))
         pack_frame(1, j)
-    frames_on(1)
+    toward(lambda d: [frame_out(1, j, d) for j in range(DEPTH)])
+    fetch(2)
 
     def block(b, _):
         pl.when(b + 2 < BLOCKS)(lambda: frames_wait(b + 2))
         receive_state(b)
         run(b, b + 1)
-        frames_on(b + 2)
+        pl.when(b + 3 < BLOCKS)(lambda: fetch(b + 3))
         return 0
 
     lax.fori_loop(0, BLOCKS - 1, block, 0)
@@ -395,7 +441,7 @@
             c_out[s, 2 * q] = both[:, 0:64]
             c_out[s, 2 * q + 1] = both[:, 64:128]
 
-    drain()
+    toward(drain)
 
 
 def write_out(h, c, h_out, c_out, sem):
@@ -420,9 +466,8 @@
             [(BLOCKS, 2, HP, OWN, 128), (BLOCKS, 8, 16, 128), (BLOCKS, 2, 16, 128)],
             [(BLOCKS, 2, OWN, 128), (BLOCKS, PAIRS // 2, 8, 128), (BLOCKS, 2, 8, 128)],
         ]
-        recv_bufs = [pltpu.VMEM(s, BF16 if k < 2 else F32) for k in range(3) for s in strips[k]]
         strips[0] = [(s[0] + 1,) + s[1:] for s in strips[0]]
-        send_bufs = [pltpu.VMEM(s, BF16 if k < 2 else F32) for k in range(3) for s in strips[k]]
+        strip_bufs = [pltpu.VMEM(s, BF16 if k < 2 else F32) for k in range(3) for s in strips[k]]
         h_pairs, c_pairs = pl.pallas_call(
             kernel,
             out_shape=(pltpu.VMEM(frames.shape, BF16), pltpu.VMEM(c_init.shape, F32)),
@@ -443,11 +488,11 @@
                 pltpu.VMEM((768, 512), BF16),
                 pltpu.VMEM((768, 512), BF16),
                 pltpu.VMEM((1, 512), F32),
-                *send_bufs, *recv_bufs,
+                *strip_bufs, *strip_bufs,
                 pltpu.SemaphoreType.DMA((DEPTH,)),
                 pltpu.SemaphoreType.DMA((5,)),
-                pltpu.SemaphoreType.DMA((3, 5)),
-                pltpu.SemaphoreType.DMA((BLOCKS, 3 + DEPTH, 5)),
+                pltpu.SemaphoreType.DMA((3 + DEPTH, 5)),
+                pltpu.SemaphoreType.DMA((BLOCKS + 1, 3 + DEPTH, 5)),
             ],
             compiler_params=pltpu.CompilerParams(collective_id=0, has_side_effects=True, vmem_limit_bytes=56 * 2**20),
         )(frames, w_x, w_h, gate_bias.reshape(1, 256), h_init, c_init)

time: 45.2 us -> 44.2 us (0.978)
  Pallas kernels: 44.4 us -> 43.4 us
    pallas_call x1, Pallas kernels: 41.3 us -> 40.3 us  [local_run(): pl.pallas_call(kernel, out_shape=(pltpu.VMEM(frames.shape, BF16), pltpu.V...]
where the time goes in v5:
time: 44.2 us; the launch traced here: 44.1 us
  Pallas kernels  43.4 us (98%)
  between operations  0.64 us (1%)
    pallas_call x1, Pallas kernels, local_run(): pl.pallas_call(kernel, out_shape=(pltpu.VMEM(frames.shape, BF16), pltpu.V...  40.3 us
    pallas_call x1, Pallas kernels, local_run(): pl.pallas_call(write_out, out_shape=(jax.ShapeDtypeStruct(frames.shape, B...  3.1 us

profile of v5, /device:TPU:0, one launch (start us, length us, event | category | flops | bytes accessed | tf_op | source)
XLA Modules:
  0.0 44.1 jit_solution(5744590917740220922)
XLA Ops:
  0.6 40.3 %shard_map.77 = (bf16[12,2,32,32,64]{4,3,2,1,0:T(8,128)(2,1)S(1)}, f32[2,32,32,64]{3,2,1,0:T(8,128)S(1)}) custom-call(bf16[12,2,32,32,64]{4,3,2,1,0:T(8,128)(2,1)} %frames.1, bf16[3,3,64,256]{3,2,1,0:T(8,128)(2,1)} %wx_hbm.1, bf16[3,3,64,256]{3,2,1,0:T(8,128)(2,1)} %wh_hbm.1, f32[1,256]{1,0:T(1,128)} %bitcast.1, bf16[2,32,32,64]{3,2,1,0:T(8,128)(2,1)} %h_hbm.1, ...), custom_call_target="tpu_custom_call" | custom-call | tf_op jit(solution)/shard_map/pallas_call | solution.py:471
  41.0 3.1 %shard_map.78 = (bf16[12,2,32,32,64]{4,3,2,1,0:T(8,128)(2,1)}, f32[2,32,32,64]{3,2,1,0:T(8,128)}) custom-call(bf16[12,2,32,32,64]{4,3,2,1,0:T(8,128)(2,1)S(1)} %get-tuple-element.4.h, f32[2,32,32,64]{3,2,1,0:T(8,128)S(1)} %get-tuple-element.5.c), custom_call_target="tpu_custom_call" | custom-call | tf_op jit(solution)/shard_map/pallas_call | solution.py:499

commit v6 on v5

--- a/solution.py
+++ b/solution.py
@@ -22,6 +22,10 @@
 FROM_UP, FROM_DOWN, FROM_SIDE, FROM_DUP, FROM_DDOWN = DIRS = range(5)
 MIRROR = (FROM_DOWN, FROM_UP, FROM_SIDE, FROM_DDOWN, FROM_DUP)
 FRAME, HID, CELL = range(3)
+MID, HALO = slice(8, 72), slice(72, 80)
+BEFORE, AFTER = slice(0, 8), slice(80, 88)
+FIRST, COWN, CHALO = slice(8, 16), slice(0, 64), slice(64, 72)
+LEFT, RIGHT = slice(0, 64), slice(64, 128)
 COL_ORDER = (0, 1, 6, 7, 2, 3, 4, 5)
 
 
@@ -83,20 +87,20 @@
         lax.fori_loop(0, PAIRS // 4, body, 0)
 
     def wrap_first(ref, q):
-        ref[q, 80:88, :] = ref[q, 8:16, :]
+        ref[q, AFTER, :] = ref[q, FIRST, :]
 
     nil = jnp.zeros((SUBL, 128), F32)
     for q in (0, 1, ROWS_ALL - 2, ROWS_ALL - 1):
         hs[q] = nil
-        for j in range(DEPTH):
+        for j in range(2 * DEPTH):
             xs[j, q] = nil
     for q in (0, PAIRS + 1):
         cs[q] = nil[0:72]
     for q in range(PAIRS):
-        cs[1 + q, 64:72, :] = nil[0:8]
-        for j in range(1, DEPTH):
-            xs[j, EDGE + q, 0:8, :] = nil[0:8]
-            xs[j, EDGE + q, 72:80, :] = nil[0:8]
+        cs[1 + q, CHALO, :] = nil[BEFORE]
+        for j in (1, 2, 4, 5):
+            xs[j, EDGE + q, BEFORE, :] = nil[BEFORE]
+            xs[j, EDGE + q, HALO, :] = nil[BEFORE]
 
     strip_at = pl.multiple_of(8 + 56 * (1 - col), 8)
     cstrip_at = pl.multiple_of(56 * (1 - col), 8)
@@ -105,8 +109,8 @@
 
     def pack_rows(src, s_row):
         for p in range(HP):
-            s_row[0, p] = src[EDGE + p, 8:72, :].astype(BF16)
-            s_row[1, p] = src[EDGE + PAIRS - HP + p, 8:72, :].astype(BF16)
+            s_row[0, p] = src[EDGE + p, MID, :].astype(BF16)
+            s_row[1, p] = src[EDGE + PAIRS - HP + p, MID, :].astype(BF16)
 
     def pack_cols(src, s_col, s_cor, part):
         for at, i in list(enumerate(COL_ORDER))[4 * part:4 * part + 4]:
@@ -119,8 +123,8 @@
                 s_cor[1] = two
 
     def pack_narrow(src, s_row, s_col, s_cor):
-        s_row[0, 0] = src[EDGE, 8:72, :].astype(BF16)
-        s_row[1, 0] = src[EDGE + PAIRS - 1, 8:72, :].astype(BF16)
+        s_row[0, 0] = src[EDGE, MID, :].astype(BF16)
+        s_row[1, 0] = src[EDGE + PAIRS - 1, MID, :].astype(BF16)
         for i in range(PAIRS // 4):
             s_col[i] = jnp.concatenate([src[EDGE + 4 * i + u, pl.ds(8 + cstrip_from, 4), :] for u in range(4)],
                                        axis=0).astype(BF16)
@@ -137,27 +141,27 @@
                 dst[EDGE + 4 * i + u, pl.ds(cstrip_to - 64, 4), :] = strip
         for which, at, there in ((0, EDGE - 1, has_up), (1, EDGE + PAIRS, has_down)):
             strip = jnp.where(there, get_row(which).astype(F32), 0.0)
-            dst[at, 8:72, :] = strip
-            dst[at, 80:88, :] = strip[0:8]
-            unpack_side(dst, at, jnp.where(there, get_cor(which).astype(F32)[0:8], 0.0))
+            dst[at, MID, :] = strip
+            dst[at, AFTER, :] = strip[BEFORE]
+            unpack_side(dst, at, jnp.where(there, get_cor(which).astype(F32)[BEFORE], 0.0))
 
     def unpack_side(dst, q, strip):
         strip = strip * col_mask
-        dst[q, 72:80, :] = strip
-        dst[q, 0:8, :] = strip
+        dst[q, HALO, :] = strip
+        dst[q, BEFORE, :] = strip
 
     def unpack_bf16(dst, get_row, get_col, get_cor):
         for at, i in enumerate(COL_ORDER):
             both = get_col(at).astype(F32)
-            unpack_side(dst, EDGE + 2 * i, both[0:8])
+            unpack_side(dst, EDGE + 2 * i, both[BEFORE])
             unpack_side(dst, EDGE + 2 * i + 1, both[8:16])
 
         for which, first, there in ((0, EDGE - HP, has_up), (1, EDGE + PAIRS, has_down)):
             both = jnp.where(there, get_cor(which).astype(F32), 0.0)
             for p in range(HP):
                 strip = jnp.where(there, get_row(which, p).astype(F32), 0.0)
-                dst[first + p, 8:72, :] = strip
-                dst[first + p, 80:88, :] = strip[0:8]
+                dst[first + p, MID, :] = strip
+                dst[first + p, AFTER, :] = strip[BEFORE]
                 at = 2 - HP + p if which == 0 else p
                 unpack_side(dst, first + p, both[8 * at:8 * at + 8])
 
@@ -231,8 +235,8 @@
 
     def send_state_rest(b):
         pack_rows(hs, sh_row.at[b])
-        sc_row[b, 0] = cs[1, 0:OWN, :]
-        sc_row[b, 1] = cs[PAIRS, 0:OWN, :]
+        sc_row[b, 0] = cs[1, COWN, :]
+        sc_row[b, 1] = cs[PAIRS, COWN, :]
         sc_cor[b, 0] = cs[1, pl.ds(cstrip_at, 8), :]
         sc_cor[b, 1] = cs[PAIRS, pl.ds(cstrip_at, 8), :]
 
@@ -250,23 +254,28 @@
             for u in range(2):
                 cs[1 + 2 * i + u, pl.ds(cstrip_to, 4), :] = rc_col[b, at, 4 * u:4 * u + 4]
         for which, at, there in ((0, 0, has_up), (1, 1 + PAIRS, has_down)):
-            cs[at, 0:OWN, :] = jnp.where(there, rc_row[b, which], 0.0)
-            cs[at, 64:72, :] = jnp.where(there, rc_cor[b, which], 0.0)
-
-    def take_frame(b, j, pairs):
-        for q in pairs:
+            cs[at, COWN, :] = jnp.where(there, rc_row[b, which], 0.0)
+            cs[at, CHALO, :] = jnp.where(there, rc_cor[b, which], 0.0)
+
+    def plane(b, j):
+        return xs.at[lax.rem(b, 2) * DEPTH + j]
+
+    def take_frame(b, j):
+        dst = plane(b, j)
+        for q in range(PAIRS):
             for s in range(2):
                 both = jnp.concatenate([fbuf[j, s, 2 * q], fbuf[j, s, 2 * q + 1]], axis=1).astype(F32)
-                xs[j, EDGE + q, pl.ds(8 + s, 32, stride=2), :] = both
-            wrap_first(xs.at[j], EDGE + q)
+                dst[EDGE + q, pl.ds(8 + s, 32, stride=2), :] = both
+            wrap_first(dst, EDGE + q)
+        pack_frame(b, j)
 
     def pack_frame(b, j):
         if j:
-            pack_narrow(xs.at[j], sx_row.at[b, j], sx_col.at[b, j], sx_cor.at[b, j])
+            pack_narrow(plane(b, j), sx_row.at[b, j], sx_col.at[b, j], sx_cor.at[b, j])
             return
-        pack_rows(xs.at[j], sx_row.at[b, j])
+        pack_rows(plane(b, j), sx_row.at[b, j])
         for part in range(2):
-            pack_cols(xs.at[j], sx_col.at[b, j], sx_cor.at[b, j], part)
+            pack_cols(plane(b, j), sx_col.at[b, j], sx_cor.at[b, j], part)
 
     def tasks(j):
         first, count, width = region(j)
@@ -295,18 +304,16 @@
 
     def unpack_frame(b, j):
         if j:
-            unpack_narrow(xs.at[j], lambda w: rx_row[b, j, w, 0], lambda i: rx_col[b, j, i], lambda w: rx_cor[b, j, w])
+            unpack_narrow(plane(b, j), lambda w: rx_row[b, j, w, 0], lambda i: rx_col[b, j, i], lambda w: rx_cor[b, j, w])
             return
-        unpack_bf16(xs.at[j], lambda w, p: rx_row[b, j, w, p], lambda i: rx_col[b, j, i], lambda w: rx_cor[b, j, w])
+        unpack_bf16(plane(b, j), lambda w, p: rx_row[b, j, w, p], lambda i: rx_col[b, j, i], lambda w: rx_cor[b, j, w])
 
     def x_gates(src, slot, task):
         j, pairs, width, at = task
         xg[j, at:at + len(pairs) * width, :] = product(src, task, wx) + bias[...]
 
     all_tasks = [t for j in range(DEPTH) for t in tasks(j)]
-    last_of_step = [i + 1 == len(all_tasks) or all_tasks[i + 1][0] != t[0] for i, t in enumerate(all_tasks)]
-
-    def frames_wait(following):
+    def frames_wait():
         for j in range(DEPTH):
             frame_copy(0, j).wait()
 
@@ -333,22 +340,22 @@
                 h_new = h_new * up_mask
             if at >= EDGE + PAIRS:
                 h_new = h_new * down_mask
-            hs[at, 8:72, :] = h_new[0:OWN]
-            hs[at, 80:88, :] = h_new[0:8]
+            hs[at, MID, :] = h_new[0:OWN]
+            hs[at, AFTER, :] = h_new[BEFORE]
             if width == 72:
                 unpack_side(hs, at, h_new[64:72])
             if EDGE <= at < EDGE + PAIRS:
                 for s in range(2):
                     both = hs[at, pl.ds(8 + s, 32, stride=2), :].astype(BF16)
-                    h_out[t, s, 2 * (at - EDGE)] = both[:, 0:64]
-                    h_out[t, s, 2 * (at - EDGE) + 1] = both[:, 64:128]
+                    h_out[t, s, 2 * (at - EDGE)] = both[:, LEFT]
+                    h_out[t, s, 2 * (at - EDGE) + 1] = both[:, RIGHT]
 
     def run(hid_block, x_block):
         todo = []
         if hid_block is not None:
             todo += [(hs, t, True) for t in all_tasks]
         if x_block is not None:
-            todo += [(xs.at[t[0]], t, False) for t in all_tasks]
+            todo += [(plane(x_block, t[0]), t, False) for t in all_tasks]
         def ahead(i):
             src, task, hidden = todo[i]
             (h_gates if hidden else x_gates)(src, i % 2, task)
@@ -363,19 +370,17 @@
                 ahead(i + 1)
             if hidden:
                 cells(i % 2, task, hid_block * DEPTH + task[0])
-                if x_block is not None and n + 2 == len(all_tasks):
+                if x_block is None:
+                    continue
+                if n < DEPTH:
+                    take_frame(x_block + 1, n)
+                if n + 2 == len(all_tasks):
                     send_state_cols(hid_block + 1, 0)
                     send_state_rest(hid_block + 1)
                     toward(lambda d: [frame_in(x_block, j, d) for j in range(DEPTH)])
-                if x_block is not None and n + 1 == len(all_tasks):
+                if n + 1 == len(all_tasks):
                     send_state_cols(hid_block + 1, 1)
-            elif last_of_step[n]:
-                take_frame(x_block + 1, task[0], range(PAIRS))
-                pack_frame(x_block + 1, task[0])
-                if task[0] == 1:
-                    toward(lambda d: [frame_out(x_block + 1, j, d) for j in (0, 1)])
-                if task[0] == 2:
-                    toward(lambda d: frame_out(x_block + 1, 2, d))
+                    toward(lambda d: [frame_out(x_block + 1, j, d) for j in range(DEPTH)])
 
     def weights(src, dst):
         zero = jnp.zeros((64, 64), BF16)
@@ -390,8 +395,7 @@
 
     for j in range(DEPTH):
         frame_copy(0, j).wait()
-        take_frame(0, j, range(PAIRS))
-        pack_frame(0, j)
+        take_frame(0, j)
         if j == 0:
             pl.semaphore_wait(barrier, 3 + 2 * (has_up & has_down).astype(jnp.int32))
         toward(lambda d: frame_out(0, j, d))
@@ -411,21 +415,19 @@
     for g in range(4):
         piece = bias_in[:, 64 * g:64 * g + 64]
         bias[:, 128 * g:128 * g + 128] = jnp.concatenate([piece, piece], axis=1)
+    frames_wait()
+    for j in range(DEPTH):
+        take_frame(1, j)
+    toward(lambda d: [frame_out(1, j, d) for j in range(DEPTH)])
+    fetch(2)
     for j in range(DEPTH):
         toward(lambda d: frame_in(0, j, d))
         unpack_frame(0, j)
-        if j == DEPTH - 1:
-            frames_wait(1)
         for task in tasks(j):
-            x_gates(xs.at[j], 0, task)
-    for j in range(DEPTH):
-        take_frame(1, j, range(PAIRS))
-        pack_frame(1, j)
-    toward(lambda d: [frame_out(1, j, d) for j in range(DEPTH)])
-    fetch(2)
+            x_gates(plane(0, j), 0, task)
 
     def block(b, _):
-        pl.when(b + 2 < BLOCKS)(lambda: frames_wait(b + 2))
+        pl.when(b + 2 < BLOCKS)(frames_wait)
         receive_state(b)
         run(b, b + 1)
         pl.when(b + 3 < BLOCKS)(lambda: fetch(b + 3))
@@ -438,8 +440,8 @@
     for q in range(PAIRS):
         for s in range(2):
             both = cs[1 + q, pl.ds(s, 32, stride=2), :]
-            c_out[s, 2 * q] = both[:, 0:64]
-            c_out[s, 2 * q + 1] = both[:, 64:128]
+            c_out[s, 2 * q] = both[:, LEFT]
+            c_out[s, 2 * q + 1] = both[:, RIGHT]
 
     toward(drain)
 
@@ -480,7 +482,7 @@
                 pltpu.VMEM((1, 256), F32),
                 pltpu.VMEM(h_init.shape, BF16),
                 pltpu.VMEM(c_init.shape, F32),
-                pltpu.VMEM((DEPTH, ROWS_ALL, SUBL, 128), F32),
+                pltpu.VMEM((2 * DEPTH, ROWS_ALL, SUBL, 128), F32),
                 pltpu.VMEM((ROWS_ALL, SUBL, 128), F32),
                 pltpu.VMEM((PAIRS + 2, 72, 128), F32),
                 pltpu.VMEM((DEPTH, most, 512), F32),

time: 44.2 us -> 42.9 us (0.971)
  Pallas kernels: 43.4 us -> 42 us
    pallas_call x1, Pallas kernels: 40.3 us -> 38.9 us  [local_run(): pl.pallas_call(kernel, out_shape=(pltpu.VMEM(frames.shape, BF16), pltpu.V...]
where the time goes in v6:
time: 42.9 us; the launch traced here: 42.8 us
  Pallas kernels  42 us (98%)
  between operations  0.8 us (2%)
    pallas_call x1, Pallas kernels, local_run(): pl.pallas_call(kernel, out_shape=(pltpu.VMEM(frames.shape, BF16), pltpu.V...  38.9 us
    pallas_call x1, Pallas kernels, local_run(): pl.pallas_call(write_out, out_shape=(jax.ShapeDtypeStruct(frames.shape, B...  3.1 us

profile of v6, /device:TPU:0, one launch (start us, length us, event | category | flops | bytes accessed | tf_op | source)
XLA Modules:
  0.0 42.8 jit_solution(7682116105332289654)
XLA Ops:
  0.6 38.9 %shard_map.77 = (bf16[12,2,32,32,64]{4,3,2,1,0:T(8,128)(2,1)S(1)}, f32[2,32,32,64]{3,2,1,0:T(8,128)S(1)}) custom-call(bf16[12,2,32,32,64]{4,3,2,1,0:T(8,128)(2,1)} %frames.1, bf16[3,3,64,256]{3,2,1,0:T(8,128)(2,1)} %wx_hbm.1, bf16[3,3,64,256]{3,2,1,0:T(8,128)(2,1)} %wh_hbm.1, f32[1,256]{1,0:T(1,128)} %bitcast.1, bf16[2,32,32,64]{3,2,1,0:T(8,128)(2,1)} %h_hbm.1, ...), custom_call_target="tpu_custom_call" | custom-call | tf_op jit(solution)/shard_map/pallas_call | solution.py:473
  39.6 3.1 %shard_map.78 = (bf16[12,2,32,32,64]{4,3,2,1,0:T(8,128)(2,1)}, f32[2,32,32,64]{3,2,1,0:T(8,128)}) custom-call(bf16[12,2,32,32,64]{4,3,2,1,0:T(8,128)(2,1)S(1)} %get-tuple-element.4.h, f32[2,32,32,64]{3,2,1,0:T(8,128)S(1)} %get-tuple-element.5.c), custom_call_target="tpu_custom_call" | custom-call | tf_op jit(solution)/shard_map/pallas_call | solution.py:501

commit v7 on v6

--- a/solution.py
+++ b/solution.py
@@ -396,11 +396,11 @@
     for j in range(DEPTH):
         frame_copy(0, j).wait()
         take_frame(0, j)
+        frame_copy(DEPTH + j, j).start()
+    for j in range(DEPTH):
         if j == 0:
             pl.semaphore_wait(barrier, 3 + 2 * (has_up & has_down).astype(jnp.int32))
         toward(lambda d: frame_out(0, j, d))
-    for j in range(DEPTH):
-        frame_copy(DEPTH + j, j).start()
     for cp in inputs:
         cp.wait()
     ingest(lambda s, r: h_in[s, r], hs.at[pl.ds(EDGE, PAIRS), pl.ds(8, OWN)])

time: 42.9 us -> 42.8 us (level)
  no operation moved by 1% of the time
where the time goes in v7:
time: 42.8 us; the launch traced here: 42.7 us
  Pallas kernels  41.9 us (98%)
  between operations  0.8 us (2%)
    pallas_call x1, Pallas kernels, local_run(): pl.pallas_call(kernel, out_shape=(pltpu.VMEM(frames.shape, BF16), pltpu.V...  38.8 us
    pallas_call x1, Pallas kernels, local_run(): pl.pallas_call(write_out, out_shape=(jax.ShapeDtypeStruct(frames.shape, B...  3.1 us

profile of v7, /device:TPU:0, one launch (start us, length us, event | category | flops | bytes accessed | tf_op | source)
XLA Modules:
  0.0 42.7 jit_solution(3726151254259179749)
XLA Ops:
  0.6 38.8 %shard_map.77 = (bf16[12,2,32,32,64]{4,3,2,1,0:T(8,128)(2,1)S(1)}, f32[2,32,32,64]{3,2,1,0:T(8,128)S(1)}) custom-call(bf16[12,2,32,32,64]{4,3,2,1,0:T(8,128)(2,1)} %frames.1, bf16[3,3,64,256]{3,2,1,0:T(8,128)(2,1)} %wx_hbm.1, bf16[3,3,64,256]{3,2,1,0:T(8,128)(2,1)} %wh_hbm.1, f32[1,256]{1,0:T(1,128)} %bitcast.1, bf16[2,32,32,64]{3,2,1,0:T(8,128)(2,1)} %h_hbm.1, ...), custom_call_target="tpu_custom_call" | custom-call | tf_op jit(solution)/shard_map/pallas_call | solution.py:473
  39.4 3.1 %shard_map.78 = (bf16[12,2,32,32,64]{4,3,2,1,0:T(8,128)(2,1)}, f32[2,32,32,64]{3,2,1,0:T(8,128)}) custom-call(bf16[12,2,32,32,64]{4,3,2,1,0:T(8,128)(2,1)S(1)} %get-tuple-element.4.h, f32[2,32,32,64]{3,2,1,0:T(8,128)S(1)} %get-tuple-element.5.c), custom_call_target="tpu_custom_call" | custom-call | tf_op jit(solution)/shard_map/pallas_call | solution.py:501

commit v8 on v7

--- a/solution.py
+++ b/solution.py
@@ -372,8 +372,8 @@
                 cells(i % 2, task, hid_block * DEPTH + task[0])
                 if x_block is None:
                     continue
-                if n < DEPTH:
-                    take_frame(x_block + 1, n)
+                if n % 2 and n < 2 * DEPTH:
+                    take_frame(x_block + 1, n // 2)
                 if n + 2 == len(all_tasks):
                     send_state_cols(hid_block + 1, 0)
                     send_state_rest(hid_block + 1)

time: 42.8 us -> 42.8 us (level)
  no operation moved by 1% of the time
where the time goes in v8:
time: 42.8 us; the launch traced here: 42.7 us
  Pallas kernels  41.9 us (98%)
  between operations  0.8 us (2%)
    pallas_call x1, Pallas kernels, local_run(): pl.pallas_call(kernel, out_shape=(pltpu.VMEM(frames.shape, BF16), pltpu.V...  38.8 us
    pallas_call x1, Pallas kernels, local_run(): pl.pallas_call(write_out, out_shape=(jax.ShapeDtypeStruct(frames.shape, B...  3.1 us

profile of v8, /device:TPU:0, one launch (start us, length us, event | category | flops | bytes accessed | tf_op | source)
XLA Modules:
  0.0 42.7 jit_solution(6777547958449895582)
XLA Ops:
  0.6 38.8 %shard_map.77 = (bf16[12,2,32,32,64]{4,3,2,1,0:T(8,128)(2,1)S(1)}, f32[2,32,32,64]{3,2,1,0:T(8,128)S(1)}) custom-call(bf16[12,2,32,32,64]{4,3,2,1,0:T(8,128)(2,1)} %frames.1, bf16[3,3,64,256]{3,2,1,0:T(8,128)(2,1)} %wx_hbm.1, bf16[3,3,64,256]{3,2,1,0:T(8,128)(2,1)} %wh_hbm.1, f32[1,256]{1,0:T(1,128)} %bitcast.1, bf16[2,32,32,64]{3,2,1,0:T(8,128)(2,1)} %h_hbm.1, ...), custom_call_target="tpu_custom_call" | custom-call | tf_op jit(solution)/shard_map/pallas_call | solution.py:473
  39.4 3.1 %shard_map.78 = (bf16[12,2,32,32,64]{4,3,2,1,0:T(8,128)(2,1)}, f32[2,32,32,64]{3,2,1,0:T(8,128)}) custom-call(bf16[12,2,32,32,64]{4,3,2,1,0:T(8,128)(2,1)S(1)} %get-tuple-element.4.h, f32[2,32,32,64]{3,2,1,0:T(8,128)S(1)} %get-tuple-element.5.c), custom_call_target="tpu_custom_call" | custom-call | tf_op jit(solution)/shard_map/pallas_call | solution.py:501
